TPU v7x, 32 devices: a whole 2x2x4 slice. The times are simulated.
32 devices in a mesh: dp: 8 (over z, x), sp: 4 (over y, core).
Axes of the slice: x: 2, y: 2, z: 4, core: 2. Of those that a mesh axis runs over, the one named last changes fastest.
Arguments:
- frames: bfloat16 [8, 1280, 1024], P('dp', 'sp'), may hold values from -6 to 6
- text: bfloat16 [8, 256, 1024], P('dp', 'sp'), may hold values from -6 to 6
- frame_len: int32 [8], P('dp'), may hold values from 1 to 1280, 7680 in all
- text_len: int32 [8], P('dp'), may hold values from 1 to 256, 1024 in all
- cotangent: bfloat16 [8, 1280, 1024], P('dp', 'sp'), may hold values from -6 to 6
- proj_query: bfloat16 [1024, 1024], P('dp'), may hold values from -0.1875 to 0.1875
- proj_key: bfloat16 [1024, 1024], P('dp'), may hold values from -0.1875 to 0.1875
- proj_value: bfloat16 [1024, 1024], P('dp'), may hold values from -0.1875 to 0.1875
- proj_out: bfloat16 [1024, 1024], P('dp'), may hold values from -1.75 to 1.75
- cross_query: bfloat16 [1024, 1024], P('dp'), may hold values from -0.1875 to 0.1875
- cross_key: bfloat16 [1024, 1024], P('dp'), may hold values from -0.1875 to 0.1875
- cross_value: bfloat16 [1024, 1024], P('dp'), may hold values from -0.1875 to 0.1875
- cross_out: bfloat16 [1024, 1024], P('dp'), may hold values from -0.5 to 0.5
- ffn_up: bfloat16 [1024, 4096], P('dp'), may hold values from -0.1875 to 0.1875
- ffn_down: bfloat16 [4096, 1024], P('dp'), may hold values from -0.09375 to 0.09375
- gain_attn: bfloat16 [1024], P('dp'), may hold values from 0.25 to 1.75
- bias_attn: bfloat16 [1024], P('dp'), may hold values from -3 to 3
- gain_cross: bfloat16 [1024], P('dp'), may hold values from 0.25 to 1.75
- bias_cross: bfloat16 [1024], P('dp'), may hold values from -3 to 3
- gain_ffn: bfloat16 [1024], P('dp'), may hold values from 0.25 to 1.75
- bias_ffn: bfloat16 [1024], P('dp'), may hold values from -3 to 3
Outputs:
- output: bfloat16 [8, 1280, 1024], P('dp', 'sp')
- grad_frames: float32 [8, 1280, 1024], P('dp', 'sp')
- grad_text: float32 [8, 256, 1024], P('dp', 'sp')
- grad_proj_query: float32 [1024, 1024], P('dp')
- grad_proj_key: float32 [1024, 1024], P('dp')
- grad_proj_value: float32 [1024, 1024], P('dp')
- grad_proj_out: float32 [1024, 1024], P('dp')
- grad_cross_query: float32 [1024, 1024], P('dp')
- grad_cross_key: float32 [1024, 1024], P('dp')
- grad_cross_value: float32 [1024, 1024], P('dp')
- grad_cross_out: float32 [1024, 1024], P('dp')
- grad_ffn_up: float32 [1024, 4096], P('dp')
- grad_ffn_down: float32 [4096, 1024], P('dp')
- grad_gain_attn: float32 [1024], P('dp')
- grad_bias_attn: float32 [1024], P('dp')
- grad_gain_cross: float32 [1024], P('dp')
- grad_bias_cross: float32 [1024], P('dp')
- grad_gain_ffn: float32 [1024], P('dp')
- grad_bias_ffn: float32 [1024], P('dp')
Inputs may be any that keep to these rules, and one draw needn't show every extreme that they name: Each clip's frames 0 to frame_len - 1 are valid; some clip has all 1280 valid. Each clip's text states 0 to text_len - 1 are valid; some clip has all 256 valid.
All inputs are finite; a program needn't handle non-finite values. No bound on the sum of `frame_len` or of `text_len` on one device may be relied on, other than what follows from the above.
Results may differ from a plain program's by a relative error of at most 0.024.
Values may be sent and summed in bfloat16 or wider, within the bound.
A program may use at most 320 MiB of HBM per device.

v0:
```python
from functools import partial

import jax
import jax.numpy as jnp
from jax import lax
from jax.sharding import PartitionSpec as P

HEAD_DIM = 64


epsilon = 1e-05
negative = -1e30


def as_sent(shard):

    def short(part):
        return part.astype(jnp.bfloat16) if part.dtype == jnp.float32 else part

    return jax.tree.map(short, shard)


def layer_norm(values, gain_vec, offset):
    centre = jnp.mean(values, axis=-1, keepdims=True)
    spread = jnp.mean(jnp.square(values - centre), axis=-1, keepdims=True)
    return (values - centre) * lax.rsqrt(spread + epsilon) * gain_vec + offset


def mat_mul(first_op, second_op):
    return jnp.dot(first_op, second_op, preferred_element_type=jnp.float32)


def mat_mul_t(first_op, second_op):
    return lax.dot_general(
        first_op, second_op, (((1,), (1,)), ((), ())), preferred_element_type=jnp.float32
    )


def mat_t_mul(first_op, second_op):
    return lax.dot_general(
        first_op, second_op, (((0,), (0,)), ((), ())), preferred_element_type=jnp.float32
    )


def causal_mask(n_rows, length):
    row_pos = lax.broadcasted_iota(jnp.int32, (n_rows, n_rows), 0)
    col_pos = lax.broadcasted_iota(jnp.int32, (n_rows, n_rows), 1)
    return (col_pos < length) & (col_pos <= row_pos)


def text_mask(n_rows, n_keys, length):
    col_pos = lax.broadcasted_iota(jnp.int32, (n_rows, n_keys), 1)
    return col_pos < length


def attend(queries, key_rows, values, visible):
    factor = HEAD_DIM ** (-0.5)
    pieces = []
    totals = []
    for head_at in range(queries.shape[1] // HEAD_DIM):
        columns = slice(head_at * HEAD_DIM, (head_at + 1) * HEAD_DIM)
        score = jnp.where(
            visible, mat_mul_t(queries[:, columns], key_rows[:, columns]) * factor, negative
        )
        row_max = jnp.max(score, axis=1, keepdims=True)
        raised = jnp.exp(score - row_max)
        summed = jnp.sum(raised, axis=1, keepdims=True)
        probs_low = (raised / summed).astype(jnp.bfloat16)
        pieces.append(mat_mul(probs_low, values[:, columns]))
        totals.append((row_max + jnp.log(summed))[:, 0])
    return (jnp.concatenate(pieces, axis=1).astype(jnp.bfloat16), jnp.stack(totals))


def attend_back(queries, key_rows, values, grad_ctx, log_sums, visible):
    factor = HEAD_DIM ** (-0.5)
    grad_qs = []
    grad_ks = []
    grad_vs = []
    for head_at in range(queries.shape[1] // HEAD_DIM):
        columns = slice(head_at * HEAD_DIM, (head_at + 1) * HEAD_DIM)
        q_part = queries[:, columns]
        k_part = key_rows[:, columns]
        d_part = grad_ctx[:, columns]
        score = jnp.where(visible, mat_mul_t(q_part, k_part) * factor, negative)
        probs = jnp.where(visible, jnp.exp(score - log_sums[head_at][:, None]), 0.0)
        grad_probs = mat_mul_t(d_part, values[:, columns])
        inner = jnp.sum(probs * grad_probs, axis=1, keepdims=True)
        grad_score = (probs * (grad_probs - inner)).astype(jnp.bfloat16)
        grad_qs.append(mat_mul(grad_score, k_part) * factor)
        grad_ks.append(mat_t_mul(grad_score, q_part) * factor)
        grad_vs.append(mat_t_mul(probs.astype(jnp.bfloat16), d_part))
    return (
        jnp.concatenate(grad_qs, axis=1).astype(jnp.bfloat16),
        jnp.concatenate(grad_ks, axis=1).astype(jnp.bfloat16),
        jnp.concatenate(grad_vs, axis=1).astype(jnp.bfloat16),
    )


def self_forward(item):
    queries, key_rows, values, length = item
    return attend(queries, key_rows, values, causal_mask(queries.shape[0], length))


def cross_forward(item):
    queries, key_rows, values, length = item
    return attend(queries, key_rows, values, text_mask(queries.shape[0], key_rows.shape[0], length))


def self_backward(item):
    queries, key_rows, values, grad_ctx, log_sums, length = item
    return attend_back(
        queries, key_rows, values, grad_ctx, log_sums, causal_mask(queries.shape[0], length)
    )


def cross_backward(item):
    queries, key_rows, values, grad_ctx, log_sums, length = item
    return attend_back(
        queries,
        key_rows,
        values,
        grad_ctx,
        log_sums,
        text_mask(queries.shape[0], key_rows.shape[0], length),
    )


def fetch(
    proj_query,
    proj_key,
    proj_value,
    proj_out,
    cross_query,
    cross_key,
    cross_value,
    cross_out,
    ffn_up,
    ffn_down,
    gain_attn,
    bias_attn,
    gain_cross,
    bias_cross,
    gain_ffn,
    bias_ffn,
):
    return (
        lax.all_gather(proj_query, "dp", axis=0, tiled=True),
        lax.all_gather(proj_key, "dp", axis=0, tiled=True),
        lax.all_gather(proj_value, "dp", axis=0, tiled=True),
        lax.all_gather(proj_out, "dp", axis=0, tiled=True),
        lax.all_gather(cross_query, "dp", axis=0, tiled=True),
        lax.all_gather(cross_key, "dp", axis=0, tiled=True),
        lax.all_gather(cross_value, "dp", axis=0, tiled=True),
        lax.all_gather(cross_out, "dp", axis=0, tiled=True),
        lax.all_gather(ffn_up, "dp", axis=0, tiled=True),
        lax.all_gather(ffn_down, "dp", axis=0, tiled=True),
        lax.all_gather(gain_attn, "dp", axis=0, tiled=True),
        lax.all_gather(bias_attn, "dp", axis=0, tiled=True),
        lax.all_gather(gain_cross, "dp", axis=0, tiled=True),
        lax.all_gather(bias_cross, "dp", axis=0, tiled=True),
        lax.all_gather(gain_ffn, "dp", axis=0, tiled=True),
        lax.all_gather(bias_ffn, "dp", axis=0, tiled=True),
    )


def to_heads(block):
    return lax.all_to_all(block, "sp", split_axis=2, concat_axis=1, tiled=True)


def to_frames(block):
    return jax.tree.map(
        lambda part, own: part.astype(own.dtype),
        lax.all_to_all(as_sent(block), "sp", split_axis=1, concat_axis=2, tiled=True),
        block,
    )


def on_device(
    frames,
    text,
    frame_len,
    text_len,
    cotangent,
    proj_query,
    proj_key,
    proj_value,
    proj_out,
    cross_query,
    cross_key,
    cross_value,
    cross_out,
    ffn_up,
    ffn_down,
    gain_attn,
    bias_attn,
    gain_cross,
    bias_cross,
    gain_ffn,
    bias_ffn,
):
    clips, local, width = frames.shape
    n_rows = clips * local
    (
        full_query,
        full_key,
        full_value,
        full_out,
        full_cquery,
        full_ckey,
        full_cvalue,
        full_cout,
        full_up,
        full_down,
        full_ga,
        full_ba,
        full_gc,
        full_bc,
        full_gf,
        full_bf,
    ) = fetch(
        proj_query,
        proj_key,
        proj_value,
        proj_out,
        cross_query,
        cross_key,
        cross_value,
        cross_out,
        ffn_up,
        ffn_down,
        gain_attn,
        bias_attn,
        gain_cross,
        bias_cross,
        gain_ffn,
        bias_ffn,
    )
    resid = frames.reshape(n_rows, width).astype(jnp.float32)
    normed1, back_one = jax.vjp(
        layer_norm, resid, full_ga.astype(jnp.float32), full_ba.astype(jnp.float32)
    )
    low_one = normed1.astype(jnp.bfloat16)
    query_rows = mat_mul(low_one, full_query).astype(jnp.bfloat16).reshape(clips, local, width)
    key_rows = mat_mul(low_one, full_key).astype(jnp.bfloat16).reshape(clips, local, width)
    value_rows = mat_mul(low_one, full_value).astype(jnp.bfloat16).reshape(clips, local, width)
    heads_q, heads_k, heads_v = (
        lax.all_to_all(query_rows, "sp", split_axis=2, concat_axis=1, tiled=True),
        lax.all_to_all(key_rows, "sp", split_axis=2, concat_axis=1, tiled=True),
        lax.all_to_all(value_rows, "sp", split_axis=2, concat_axis=1, tiled=True),
    )
    heads_ctx, sums_self = lax.map(self_forward, (heads_q, heads_k, heads_v, frame_len))
    context = to_frames(heads_ctx).reshape(n_rows, width)
    middle = resid + mat_mul(context, full_out)
    normed2, back_two = jax.vjp(
        layer_norm, middle, full_gc.astype(jnp.float32), full_bc.astype(jnp.float32)
    )
    low_two = normed2.astype(jnp.bfloat16)
    heads_q2 = to_heads(
        mat_mul(low_two, full_cquery).astype(jnp.bfloat16).reshape(clips, local, width)
    )
    text_flat = text.reshape(-1, width)
    text_k = mat_mul(text_flat, full_ckey).astype(jnp.bfloat16).reshape(text.shape)
    text_v = mat_mul(text_flat, full_cvalue).astype(jnp.bfloat16).reshape(text.shape)
    heads_k2, heads_v2 = (
        lax.all_to_all(text_k, "sp", split_axis=2, concat_axis=1, tiled=True),
        lax.all_to_all(text_v, "sp", split_axis=2, concat_axis=1, tiled=True),
    )
    heads_ctx2, sums_cross = lax.map(cross_forward, (heads_q2, heads_k2, heads_v2, text_len))
    context2 = to_frames(heads_ctx2).reshape(n_rows, width)
    after = middle + mat_mul(context2, full_cout)
    normed3, back_three = jax.vjp(
        layer_norm, after, full_gf.astype(jnp.float32), full_bf.astype(jnp.float32)
    )
    low_three = normed3.astype(jnp.bfloat16)
    hidden_pre = mat_mul(low_three, full_up)
    hidden, back_gelu = jax.vjp(partial(jax.nn.gelu, approximate=False), hidden_pre)
    hidden_low = hidden.astype(jnp.bfloat16)
    output = (after + mat_mul(hidden_low, full_down)).astype(jnp.bfloat16).reshape(frames.shape)
    (
        full_query,
        full_key,
        full_value,
        full_out,
        full_cquery,
        full_ckey,
        full_cvalue,
        full_cout,
        full_up,
        full_down,
        full_ga,
        full_ba,
        full_gc,
        full_bc,
        full_gf,
        full_bf,
    ) = fetch(
        proj_query,
        proj_key,
        proj_value,
        proj_out,
        cross_query,
        cross_key,
        cross_value,
        cross_out,
        ffn_up,
        ffn_down,
        gain_attn,
        bias_attn,
        gain_cross,
        bias_cross,
        gain_ffn,
        bias_ffn,
    )
    grad_rows = cotangent.reshape(n_rows, width)
    part_down = mat_t_mul(hidden_low, grad_rows)
    grad_hidden = back_gelu(mat_mul_t(grad_rows, full_down))[0].astype(jnp.bfloat16)
    part_up = mat_t_mul(low_three, grad_hidden)
    grad_after, part_gf, part_bf = back_three(mat_mul_t(grad_hidden, full_up))
    grad_after = grad_after + grad_rows.astype(jnp.float32)
    branch_two = grad_after.astype(jnp.bfloat16)
    part_cout = mat_t_mul(context2, branch_two)
    grad_ctx2 = to_heads(
        mat_mul_t(branch_two, full_cout).astype(jnp.bfloat16).reshape(clips, local, width)
    )
    grad_hq2, grad_hk2, grad_hv2 = lax.map(
        cross_backward, (heads_q2, heads_k2, heads_v2, grad_ctx2, sums_cross, text_len)
    )
    grad_q2 = to_frames(grad_hq2).reshape(n_rows, width)
    part_cquery = mat_t_mul(low_two, grad_q2)
    grad_tk, grad_tv = (
        lax.all_to_all(as_sent(grad_hk2), "sp", split_axis=1, concat_axis=2, tiled=True).astype(
            grad_hk2.dtype
        ),
        lax.all_to_all(as_sent(grad_hv2), "sp", split_axis=1, concat_axis=2, tiled=True).astype(
            grad_hv2.dtype
        ),
    )
    flat_k = grad_tk.reshape(-1, width)
    flat_v = grad_tv.reshape(-1, width)
    part_ckey = mat_t_mul(text_flat, flat_k)
    part_cvalue = mat_t_mul(text_flat, flat_v)
    grad_text = (mat_mul_t(flat_k, full_ckey) + mat_mul_t(flat_v, full_cvalue)).reshape(text.shape)
    grad_mid, part_gc, part_bc = back_two(mat_mul_t(grad_q2, full_cquery))
    grad_mid = grad_mid + grad_after
    branch_one = grad_mid.astype(jnp.bfloat16)
    part_out = mat_t_mul(context, branch_one)
    grad_ctx = to_heads(
        mat_mul_t(branch_one, full_out).astype(jnp.bfloat16).reshape(clips, local, width)
    )
    grad_hq, grad_hk, grad_hv = lax.map(
        self_backward, (heads_q, heads_k, heads_v, grad_ctx, sums_self, frame_len)
    )
    grad_q, grad_k, grad_v = (
        lax.all_to_all(as_sent(grad_hq), "sp", split_axis=1, concat_axis=2, tiled=True).astype(
            grad_hq.dtype
        ),
        lax.all_to_all(as_sent(grad_hk), "sp", split_axis=1, concat_axis=2, tiled=True).astype(
            grad_hk.dtype
        ),
        lax.all_to_all(as_sent(grad_hv), "sp", split_axis=1, concat_axis=2, tiled=True).astype(
            grad_hv.dtype
        ),
    )
    flat_q = grad_q.reshape(n_rows, width)
    flat_kk = grad_k.reshape(n_rows, width)
    flat_vv = grad_v.reshape(n_rows, width)
    part_query = mat_t_mul(low_one, flat_q)
    part_key = mat_t_mul(low_one, flat_kk)
    part_value = mat_t_mul(low_one, flat_vv)
    grad_normed = (
        mat_mul_t(flat_q, full_query)
        + mat_mul_t(flat_kk, full_key)
        + mat_mul_t(flat_vv, full_value)
    )
    grad_in, part_ga, part_ba = back_one(grad_normed)
    grad_frames = (grad_in + grad_mid).reshape(frames.shape)
    (
        sum_query,
        sum_key,
        sum_value,
        sum_out,
        sum_cquery,
        sum_ckey,
        sum_cvalue,
        sum_cout,
        sum_up,
        sum_down,
        sum_ga,
        sum_ba,
        sum_gc,
        sum_bc,
        sum_gf,
        sum_bf,
    ) = (
        lax.psum_scatter(
            part_query.astype(jnp.bfloat16), "dp", scatter_dimension=0, tiled=True
        ).astype(jnp.float32),
        lax.psum_scatter(
            part_key.astype(jnp.bfloat16), "dp", scatter_dimension=0, tiled=True
        ).astype(jnp.float32),
        lax.psum_scatter(
            part_value.astype(jnp.bfloat16), "dp", scatter_dimension=0, tiled=True
        ).astype(jnp.float32),
        lax.psum_scatter(
            part_out.astype(jnp.bfloat16), "dp", scatter_dimension=0, tiled=True
        ).astype(jnp.float32),
        lax.psum_scatter(
            part_cquery.astype(jnp.bfloat16), "dp", scatter_dimension=0, tiled=True
        ).astype(jnp.float32),
        lax.psum_scatter(
            part_ckey.astype(jnp.bfloat16), "dp", scatter_dimension=0, tiled=True
        ).astype(jnp.float32),
        lax.psum_scatter(
            part_cvalue.astype(jnp.bfloat16), "dp", scatter_dimension=0, tiled=True
        ).astype(jnp.float32),
        lax.psum_scatter(
            part_cout.astype(jnp.bfloat16), "dp", scatter_dimension=0, tiled=True
        ).astype(jnp.float32),
        lax.psum_scatter(
            part_up.astype(jnp.bfloat16), "dp", scatter_dimension=0, tiled=True
        ).astype(jnp.float32),
        lax.psum_scatter(
            part_down.astype(jnp.bfloat16), "dp", scatter_dimension=0, tiled=True
        ).astype(jnp.float32),
        lax.psum_scatter(
            part_ga.astype(jnp.bfloat16), "dp", scatter_dimension=0, tiled=True
        ).astype(jnp.float32),
        lax.psum_scatter(
            part_ba.astype(jnp.bfloat16), "dp", scatter_dimension=0, tiled=True
        ).astype(jnp.float32),
        lax.psum_scatter(
            part_gc.astype(jnp.bfloat16), "dp", scatter_dimension=0, tiled=True
        ).astype(jnp.float32),
        lax.psum_scatter(
            part_bc.astype(jnp.bfloat16), "dp", scatter_dimension=0, tiled=True
        ).astype(jnp.float32),
        lax.psum_scatter(
            part_gf.astype(jnp.bfloat16), "dp", scatter_dimension=0, tiled=True
        ).astype(jnp.float32),
        lax.psum_scatter(
            part_bf.astype(jnp.bfloat16), "dp", scatter_dimension=0, tiled=True
        ).astype(jnp.float32),
    )
    totals = (
        lax.psum(sum_query.astype(jnp.bfloat16), "sp").astype(jnp.float32),
        lax.psum(sum_key.astype(jnp.bfloat16), "sp").astype(jnp.float32),
        lax.psum(sum_value.astype(jnp.bfloat16), "sp").astype(jnp.float32),
        lax.psum(sum_out.astype(jnp.bfloat16), "sp").astype(jnp.float32),
        lax.psum(sum_cquery.astype(jnp.bfloat16), "sp").astype(jnp.float32),
        lax.psum(sum_ckey.astype(jnp.bfloat16), "sp").astype(jnp.float32),
        lax.psum(sum_cvalue.astype(jnp.bfloat16), "sp").astype(jnp.float32),
        lax.psum(sum_cout.astype(jnp.bfloat16), "sp").astype(jnp.float32),
        lax.psum(sum_up.astype(jnp.bfloat16), "sp").astype(jnp.float32),
        lax.psum(sum_down.astype(jnp.bfloat16), "sp").astype(jnp.float32),
        lax.psum(sum_ga.astype(jnp.bfloat16), "sp").astype(jnp.float32),
        lax.psum(sum_ba.astype(jnp.bfloat16), "sp").astype(jnp.float32),
        lax.psum(sum_gc.astype(jnp.bfloat16), "sp").astype(jnp.float32),
        lax.psum(sum_bc.astype(jnp.bfloat16), "sp").astype(jnp.float32),
        lax.psum(sum_gf.astype(jnp.bfloat16), "sp").astype(jnp.float32),
        lax.psum(sum_bf.astype(jnp.bfloat16), "sp").astype(jnp.float32),
    )
    return (output, grad_frames, grad_text) + tuple(totals)


def solution(mesh):
    placed = (
        P("dp", "sp", None),
        P("dp", "sp", None),
        P("dp"),
        P("dp"),
        P("dp", "sp", None),
        P("dp", None),
        P("dp", None),
        P("dp", None),
        P("dp", None),
        P("dp", None),
        P("dp", None),
        P("dp", None),
        P("dp", None),
        P("dp", None),
        P("dp", None),
        P("dp"),
        P("dp"),
        P("dp"),
        P("dp"),
        P("dp"),
        P("dp"),
    )
    return jax.shard_map(
        on_device,
        mesh=mesh,
        in_specs=placed,
        out_specs=(
            P("dp", "sp", None),
            P("dp", "sp", None),
            P("dp", "sp", None),
            P("dp", None),
            P("dp", None),
            P("dp", None),
            P("dp", None),
            P("dp", None),
            P("dp", None),
            P("dp", None),
            P("dp", None),
            P("dp", None),
            P("dp", None),
            P("dp"),
            P("dp"),
            P("dp"),
            P("dp"),
            P("dp"),
            P("dp"),
        ),
        check_vma=False,
    )
```

profile of v0, /device:TPU:0, one launch (start us, length us, event | category | flops | bytes accessed | tf_op | source)
XLA Modules:
  0.0 1715.3 jit_solution(14567446865710059927)
XLA Ops:
  13.4 22.3 %all-gather = bf16[8,1,128]{2,1,0:T(2,128)(2,1)S(1)} all-gather(bf16[1,1,128]{2,1,0:T(2,128)(2,1)S(1)} %bitcast.510), channel_id=1, replica_groups=mesh['dp'=8,'sp'=4] {'dp'}, dimensions={0}, use_global_device_ids=true | all-gather | bytes 2304 | tf_op jit(solution)/shard_map/all_gather | solution.py:157
  35.7 16.7 all-gather.1
  53.0 9.1 all-gather.17.cloned.1.call-done
  79.3 32.6 %all-gather.19.cloned.1.call-done = bf16[1024,1024]{1,0:T(8,128)(2,1)} async-done(((bf16[128,1024]{1,0:T(8,128)(2,1)}), bf16[1024,1024]{1,0:T(8,128)(2,1)}) %all-gather.19.cloned.1.call-update) | async-done | bytes 2097168 | tf_op jit(solution)/shard_map/all_gather | solution.py:148
  129.5 32.1 %all-gather.21.cloned.1.call-done = bf16[1024,1024]{1,0:T(8,128)(2,1)} async-done(((bf16[128,1024]{1,0:T(8,128)(2,1)}), bf16[1024,1024]{1,0:T(8,128)(2,1)}) %all-gather.21.cloned.1.call-update) | async-done | bytes 2097168 | tf_op jit(solution)/shard_map/all_gather | solution.py:149
  244.9 18.5 %all-gather.2 = bf16[8,1,128]{2,1,0:T(2,128)(2,1)S(1)} all-gather(bf16[1,1,128]{2,1,0:T(2,128)(2,1)S(1)} %bitcast.512), channel_id=1, replica_groups=mesh['dp'=8,'sp'=4] {'dp'}, dimensions={0}, use_global_device_ids=true | all-gather | bytes 2304 | tf_op jit(solution)/shard_map/all_gather | solution.py:159
  263.5 16.4 all-gather.3
  296.0 14.6 all-gather.23.cloned.1.call-done
  317.3 43.1 %all-gather.25.cloned.1.call-done = bf16[1024,1024]{1,0:T(8,128)(2,1)} async-done(((bf16[128,1024]{1,0:T(8,128)(2,1)}), bf16[1024,1024]{1,0:T(8,128)(2,1)}) %all-gather.25.cloned.1.call-update) | async-done | bytes 2097168 | tf_op jit(solution)/shard_map/all_gather | solution.py:151
  417.1 18.8 %all-gather.4 = bf16[8,1,128]{2,1,0:T(2,128)(2,1)S(1)} all-gather(bf16[1,1,128]{2,1,0:T(2,128)(2,1)S(1)} %bitcast.514), channel_id=1, replica_groups=mesh['dp'=8,'sp'=4] {'dp'}, dimensions={0}, use_global_device_ids=true | all-gather | bytes 2304 | tf_op jit(solution)/shard_map/all_gather | solution.py:161
  436.4 17.0 all-gather.5
  463.1 72.4 %all-gather.33.cloned.1.call-done = bf16[1024,4096]{1,0:T(8,128)(2,1)} async-done(((bf16[128,4096]{1,0:T(8,128)(2,1)}), bf16[1024,4096]{1,0:T(8,128)(2,1)}) %all-gather.33.cloned.1.call-update) | async-done | bytes 8388624 | tf_op jit(solution)/shard_map/all_gather | solution.py:155
  535.4 17.7 %multiply_convert_fusion.4 = (bf16[320,4096]{1,0:T(8,128)(2,1)}, f32[320,4096]{1,0:T(8,128)}, f32[320,4096]{1,0:T(8,128)}) fusion(bf16[1024,4096]{1,0:T(8,128)(2,1)} %all-gather.33.cloned.1.call-done, f32[320,1024]{1,0:T(8,128)S(1)} %get-tuple-element.268, f32[1024]{0:T(1024)} %bitcast.506, f32[1024]{0:T(1024)} %bitcast.492, f32[320]{0:T(512)} %fusion.248, ...), kind=kOutput, calls=%fused_computation.39 | convolution fusion | flops 2771189760 | bytes 22817280 | tf_op jit(solution)/shard_map/dot_general | solution.py:30
  553.1 107.0 %all-gather.35.cloned.1.call-done = bf16[4096,1024]{1,0:T(8,128)(2,1)} async-done(((bf16[512,1024]{1,0:T(8,128)(2,1)}), bf16[4096,1024]{1,0:T(8,128)(2,1)}) %all-gather.35.cloned.1.call-update) | async-done | bytes 8388624 | tf_op jit(solution)/shard_map/all_gather | solution.py:156
  660.1 12.6 add_convert_fusion
  699.2 8.9 all-to-all-done.8
  783.5 12.8 all_to_all.242
  878.3 20.0 %multiply_reduce_fusion.3 = (f32[1280]{0:T(1024)S(1)}, f32[1280]{0:T(1024)S(1)}, f32[1280]{0:T(1024)S(1)}, f32[1280]{0:T(1024)S(1)}, f32[1280,1280]{0,1:T(8,128)}) fusion(f32[1280,1280]{0,1:T(8,128)} %get-tuple-element.256, f32[1280]{0:T(1024)S(1)} %get-tuple-element.282, pred[1280]{0:T(1024)(128)(4,1)S(1)} %copy-done.114, f32[1280,1280]{0,1:T(8,128)} %fusion.171, ...), kind=kOutput, calls=%fused_computation.21 | convolution fusion | flops 239201280 | bytes 53139456 | tf_op jit(solution)/shard_map/while/body/eval_jaxpr/dot_general | solution.py:34
  903.7 22.2 %multiply_convert_fusion.3 = (bf16[1280,1280]{0,1:T(8,128)(2,1)}, bf16[1280,1280]{0,1:T(8,128)(2,1)}, bf16[1280,1280]{0,1:T(8,128)(2,1)S(1)}, bf16[1280,1280]{0,1:T(8,128)(2,1)S(1)}) fusion(f32[1280,1280]{0,1:T(8,128)} %get-tuple-element.273, f32[1280]{0:T(1024)S(1)} %get-tuple-element.209, f32[1280,1280]{0,1:T(8,128)} %get-tuple-element.256, ...), kind=kLoop, calls=%fused_computation.20 | loop fusion | flops 36044800 | bytes 65578240 | tf_op jit(solution)/shard_map/while/body/eval_jaxpr/convert_element_type | solution.py:88
  938.4 8.8 reduce.13
  949.9 14.4 all_to_all.243
  989.8 12.6 all_to_all.244
  1008.4 8.8 convolution_convert_fusion.1
  1018.3 8.6 convolution_convert_fusion
  1041.3 53.3 %reduce-scatter.21.cloned.1.call-done = bf16[128,1024]{1,0:T(8,128)(2,1)} async-done(((bf16[1024,1024]{1,0:T(8,128)(2,1)}), bf16[128,1024]{1,0:T(8,128)(2,1)}) %reduce-scatter.21.cloned.1.call-update) | async-done | bytes 262160 | tf_op jit(solution)/shard_map/reduce_scatter | solution.py:404
  1094.7 70.7 %reduce-scatter.19.cloned.1.call-done = bf16[128,1024]{1,0:T(8,128)(2,1)} async-done(((bf16[1024,1024]{1,0:T(8,128)(2,1)}), bf16[128,1024]{1,0:T(8,128)(2,1)}) %reduce-scatter.19.cloned.1.call-update) | async-done | bytes 262160 | tf_op jit(solution)/shard_map/reduce_scatter | solution.py:401
  1165.4 70.8 %reduce-scatter.17.cloned.1.call-done = bf16[128,1024]{1,0:T(8,128)(2,1)} async-done(((bf16[1024,1024]{1,0:T(8,128)(2,1)}), bf16[128,1024]{1,0:T(8,128)(2,1)}) %reduce-scatter.17.cloned.1.call-update) | async-done | bytes 262160 | tf_op jit(solution)/shard_map/reduce_scatter | solution.py:398
  1236.2 71.4 %reduce-scatter.15.cloned.1.call-done = bf16[128,1024]{1,0:T(8,128)(2,1)} async-done(((bf16[1024,1024]{1,0:T(8,128)(2,1)}), bf16[128,1024]{1,0:T(8,128)(2,1)}) %reduce-scatter.15.cloned.1.call-update) | async-done | bytes 262160 | tf_op jit(solution)/shard_map/reduce_scatter | solution.py:395
  1307.5 150.1 %reduce-scatter.27.cloned.1.call-done = bf16[128,4096]{1,0:T(8,128)(2,1)} async-done(((bf16[1024,4096]{1,0:T(8,128)(2,1)}), bf16[128,4096]{1,0:T(8,128)(2,1)}) %reduce-scatter.27.cloned.1.call-update) | async-done | bytes 1048592 | tf_op jit(solution)/shard_map/reduce_scatter | solution.py:419
  1457.7 150.1 %reduce-scatter.29.cloned.1.call-done = bf16[512,1024]{1,0:T(8,128)(2,1)} async-done(((bf16[4096,1024]{1,0:T(8,128)(2,1)}), bf16[512,1024]{1,0:T(8,128)(2,1)}) %reduce-scatter.29.cloned.1.call-update) | async-done | bytes 1048592 | tf_op jit(solution)/shard_map/reduce_scatter | solution.py:422
  1616.9 35.2 %all-reduce.6 = (bf16[1024]{0:T(1024)(128)(2,1)S(1)}, bf16[1024]{0:T(1024)(128)(2,1)S(1)}, bf16[1024]{0:T(1024)(128)(2,1)S(1)}, bf16[1024]{0:T(1024)(128)(2,1)S(...) all-reduce(bf16[1024]{0:T(1024)(128)(2,1)S(1)} %get-tuple-element.2, ...), channel_id=12, replica_groups=mesh['dp'=8,'sp'=4] {'dp'}, use_global_device_ids=true, to_apply=%region_60.61.clone | all-reduce | flops 6144 | bytes 24576
  1663.1 33.1 %all-reduce.11.cloned.1.call-done = (bf16[128,1024]{0,1:T(8,128)(2,1)}, bf16[128,1024]{0,1:T(8,128)(2,1)}, bf16[128,1024]{1,0:T(8,128)(2,1)}, bf16[128,1024]{1,0...) async-done(((bf16[128,1024]{0,1:T(8,128)(2,1)}, ...) | async-done | bytes 4194320 | tf_op jit(solution)/shard_map/psum | solution.py:450
  (668 shorter events, 493.4 us)
Async XLA Ops:
  7.2 54.9 %all-gather.17.cloned.1.call-start = ((), (), s32[]{:S(2)}) async-start(), calls=%async_computation.26 | async-start | bytes 2359296 | tf_op jit(solution)/shard_map/all_gather | solution.py:147
  8.0 103.9 %all-gather.19.cloned.1.call-start = ((), (), s32[]{:S(2)}) async-start(), calls=%async_computation.27 | async-start | bytes 2359296 | tf_op jit(solution)/shard_map/all_gather | solution.py:148
  8.7 152.9 %all-gather.21.cloned.1.call-start = ((), (), s32[]{:S(2)}) async-start(), calls=%async_computation.28 | async-start | bytes 2359296 | tf_op jit(solution)/shard_map/all_gather | solution.py:149
  9.5 270.5 %all-gather.27.cloned.1.call-start = ((), (), s32[]{:S(2)}) async-start(), calls=%async_computation.31 | async-start | bytes 2359296 | tf_op jit(solution)/shard_map/all_gather | solution.py:152
  10.0 275.6 %all-gather.29.cloned.1.call-start = ((), (), s32[]{:S(2)}) async-start(), calls=%async_computation.32 | async-start | bytes 2359296 | tf_op jit(solution)/shard_map/all_gather | solution.py:153
  10.6 300.0 %all-gather.23.cloned.1.call-start = ((), (), s32[]{:S(2)}) async-start(), calls=%async_computation.29 | async-start | bytes 2359296 | tf_op jit(solution)/shard_map/all_gather | solution.py:150
  11.2 349.2 %all-gather.25.cloned.1.call-start = ((), (), s32[]{:S(2)}) async-start(), calls=%async_computation.30 | async-start | bytes 2359296 | tf_op jit(solution)/shard_map/all_gather | solution.py:151
  11.9 446.2 %all-gather.31.cloned.1.call-start = ((), (), s32[]{:S(2)}) async-start(), calls=%async_computation.33 | async-start | bytes 2359296 | tf_op jit(solution)/shard_map/all_gather | solution.py:154
  12.7 522.7 %all-gather.33.cloned.1.call-start = ((), (), s32[]{:S(2)}) async-start(), calls=%async_computation.34 | async-start | bytes 9437184 | tf_op jit(solution)/shard_map/all_gather | solution.py:155
  74.8 49.3 %all-to-all-start = ((bf16[4,2,40960]{2,1,0:T(2,128)(2,1)}), bf16[4,2,40960]{2,1,0:T(2,128)(2,1)}, u32[]{:S(2)}, u32[]{:S(2)}) async-start(bf16[4,2,40960]{2,1,0:T(2,128)(2,1)} %reshape.960), calls=%async_computation | async-start | bytes 1310720 | tf_op jit(solution)/shard_map/all_to_all | solution.py:247
  124.1 53.7 %all-to-all-start.1 = ((bf16[4,2,40960]{2,1,0:T(2,128)(2,1)}), bf16[4,2,40960]{2,1,0:T(2,128)(2,1)}, u32[]{:S(2)}, u32[]{:S(2)}) async-start(bf16[4,2,40960]{2,1,0:T(2,128)(2,1)} %reshape.958), calls=%async_computation.1 | async-start | bytes 1310720 | tf_op jit(solution)/shard_map/all_to_all | solution.py:248
  128.3 531.8 %all-gather.35.cloned.1.call-start = ((), (), s32[]{:S(2)}) async-start(), calls=%async_computation.35 | async-start | bytes 9437184 | tf_op jit(solution)/shard_map/all_gather | solution.py:156
  177.8 27.1 %all-to-all-start.2 = ((bf16[4,2,40960]{2,1,0:T(2,128)(2,1)}), bf16[4,2,40960]{2,1,0:T(2,128)(2,1)}, u32[]{:S(2)}, u32[]{:S(2)}) async-start(bf16[4,2,40960]{2,1,0:T(2,128)(2,1)} %reshape.962), calls=%async_computation.2 | async-start | bytes 1310720 | tf_op jit(solution)/shard_map/all_to_all | solution.py:249
  241.4 49.8 %all-to-all-start.3 = ((bf16[4,2,40960]{2,1,0:T(2,128)(2,1)}), bf16[4,2,40960]{2,1,0:T(2,128)(2,1)S(1)}, u32[]{:S(2)}, u32[]{:S(2)}) async-start(bf16[4,2,40960]{2,1,0:T(2,128)(2,1)} %reshape.964), calls=%async_computation.3 | async-start | bytes 1310720 | tf_op jit(solution)/shard_map/all_to_all | solution.py:173
  291.3 22.3 %all-to-all-start.5 = ((bf16[4,2,8192]{2,1,0:T(2,128)(2,1)}), bf16[4,2,8192]{2,1,0:T(2,128)(2,1)S(1)}, u32[]{:S(2)}, u32[]{:S(2)}) async-start(bf16[4,2,8192]{2,1,0:T(2,128)(2,1)} %reshape.968), calls=%async_computation.5 | async-start | bytes 262144 | tf_op jit(solution)/shard_map/all_to_all | solution.py:265
  313.5 60.5 %all-to-all-start.6 = ((bf16[4,2,8192]{2,1,0:T(2,128)(2,1)}), bf16[4,2,8192]{2,1,0:T(2,128)(2,1)S(1)}, u32[]{:S(2)}, u32[]{:S(2)}) async-start(bf16[4,2,8192]{2,1,0:T(2,128)(2,1)} %reshape.970), calls=%async_computation.6 | async-start | bytes 262144 | tf_op jit(solution)/shard_map/all_to_all | solution.py:266
  374.1 13.8 all-to-all-start.4
  412.8 41.2 %all-to-all-start.7 = ((bf16[4,2,40960]{2,1,0:T(2,128)(2,1)}), bf16[4,2,40960]{2,1,0:T(2,128)(2,1)}, u32[]{:S(2)}, u32[]{:S(2)}) async-start(bf16[4,2,40960]{2,1,0:T(2,128)(2,1)} %reshape.972), calls=%async_computation.7 | async-start | bytes 1310720 | tf_op jit(solution)/shard_map/all_to_all | solution.py:173
  694.4 13.7 all-to-all-start.8
  697.9 339.9 %reduce-scatter.33.cloned.1.call-start = ((), (), s32[]{:S(2)}) async-start(), calls=%async_computation.45 | async-start | bytes 2359296
  744.8 294.7 %reduce-scatter.31.cloned.1.call-start = ((), (), s32[]{:S(2)}) async-start(), calls=%async_computation.44 | async-start | bytes 2359296
  768.0 273.3 %reduce-scatter.25.cloned.1.call-start = ((), (), s32[]{:S(2)}) async-start(), calls=%async_computation.41 | async-start | bytes 2359296 | tf_op jit(solution)/shard_map/reduce_scatter | solution.py:416
  772.1 269.2 %reduce-scatter.23.cloned.1.call-start = ((), (), s32[]{:S(2)}) async-start(), calls=%async_computation.40 | async-start | bytes 2359296 | tf_op jit(solution)/shard_map/reduce_scatter | solution.py:407
  822.4 13.7 all-to-all-start.10
  825.9 268.8 %reduce-scatter.21.cloned.1.call-start = ((), (), s32[]{:S(2)}) async-start(), calls=%async_computation.39 | async-start | bytes 2359296 | tf_op jit(solution)/shard_map/reduce_scatter | solution.py:404
  863.1 35.2 %all-to-all-start.13 = ((bf16[4,2,40960]{2,1,0:T(2,128)(2,1)}), bf16[4,2,40960]{2,1,0:T(2,128)(2,1)S(1)}, u32[]{:S(2)}, u32[]{:S(2)}) async-start(bf16[4,2,40960]{2,1,0:T(2,128)(2,1)} %reshape.988), calls=%async_computation.13 | async-start | bytes 1310720 | tf_op jit(solution)/shard_map/all_to_all | solution.py:360
  866.6 298.8 %reduce-scatter.19.cloned.1.call-start = ((), (), s32[]{:S(2)}) async-start(), calls=%async_computation.38 | async-start | bytes 2359296 | tf_op jit(solution)/shard_map/reduce_scatter | solution.py:401
  903.4 332.7 %reduce-scatter.17.cloned.1.call-start = ((), (), s32[]{:S(2)}) async-start(), calls=%async_computation.37 | async-start | bytes 2359296 | tf_op jit(solution)/shard_map/reduce_scatter | solution.py:398
  973.7 333.8 %reduce-scatter.15.cloned.1.call-start = ((), (), s32[]{:S(2)}) async-start(), calls=%async_computation.36 | async-start | bytes 2359296 | tf_op jit(solution)/shard_map/reduce_scatter | solution.py:395
  1007.1 450.6 %reduce-scatter.27.cloned.1.call-start = ((), (), s32[]{:S(2)}) async-start(), calls=%async_computation.42 | async-start | bytes 9437184 | tf_op jit(solution)/shard_map/reduce_scatter | solution.py:419
  1017.2 590.5 %reduce-scatter.29.cloned.1.call-start = ((), (), s32[]{:S(2)}) async-start(), calls=%async_computation.43 | async-start | bytes 9437184 | tf_op jit(solution)/shard_map/reduce_scatter | solution.py:422
  1027.0 669.2 %all-reduce.11.cloned.1.call-start = ((), (), s32[]{:S(2)}) async-start(), calls=%async_computation.46 | async-start | bytes 8388608 | tf_op jit(solution)/shard_map/psum | solution.py:450
  (163 other events, 2287.1 us)
Sparse Core Ops, SparseCore 0:
  10.2 51.8 all-gather.16
  64.2 47.6 all-gather.18
  114.0 47.6 all-gather.20
  163.6 47.6 all-gather.26
  213.3 47.6 all-gather.28
  263.0 47.6 all-gather.22
  312.8 47.6 all-gather.24
  362.5 47.5 all-gather.30
  412.3 123.0 all-gather.32
  537.4 122.6 all-gather.34
  744.9 65.6 reduce-scatter.32
  814.6 67.4 reduce-scatter.30
  885.6 67.5 reduce-scatter.24
  956.6 67.3 reduce-scatter.22
  1027.4 67.1 reduce-scatter.20
  1098.0 67.3 reduce-scatter.18
  1168.8 67.3 reduce-scatter.16
  1240.1 67.3 reduce-scatter.14
  1311.2 146.4 reduce-scatter.26
  1461.1 146.5 reduce-scatter.28
  1611.4 84.7 all-reduce.10
where the time goes:
time: 1730 us; the launch traced here: 1720 us
  waiting for transfers between devices  940 us (54%)
  blocking collectives  206 us (12%)
  matrix products  205 us (12%)
  local copies, waits for them, and re-layouts  154 us (9%)
  other arithmetic  146 us (8%)
  starting transfers between devices  44.8 us (3%)
  between operations  19.2 us (1%)
    reduce_scatter x1, waiting for transfers between devices, on_device(): lax.psum_scatter(part_up.astype(jnp.bfloat16), 'dp', scatter_dimension=0,...  150 us
    reduce_scatter x1, waiting for transfers between devices, on_device(): lax.psum_scatter(part_down.astype(jnp.bfloat16), 'dp', scatter_dimension=...  150 us
    all_gather x1, waiting for transfers between devices, fetch(): lax.all_gather(ffn_down, 'dp', axis=0, tiled=True)  107 us
    unnamed x394, local copies, waits for them, and re-layouts  101 us
    unnamed x22, other arithmetic  90.1 us
    dot_general x26, matrix products, mat_mul_t(): lax.dot_general(first_op, second_op, (((1,), (1,)), ((), ())), preferred_...  86 us
    all_gather x1, waiting for transfers between devices, fetch(): lax.all_gather(ffn_up, 'dp', axis=0, tiled=True)  72.4 us
    reduce_scatter x1, waiting for transfers between devices, on_device(): lax.psum_scatter(part_query.astype(jnp.bfloat16), 'dp', scatter_dimension...  71.4 us
  transfers between devices with their start and end apart: 32, of which 17 were waited for; matrix products, arithmetic and copies ran while one was open for 24% of the time, Pallas kernels for 0%

commit v1 on v0

v1 whole, which is shorter than its diff:
```python
from functools import partial

import jax
import jax.numpy as jnp
from jax import lax
from jax.sharding import PartitionSpec as P

HEAD_DIM = 64
EPS = 1e-05
NEGATIVE = -1e30
BF = jnp.bfloat16
F32 = jnp.float32


def mm(a, b):
    return jnp.dot(a, b, preferred_element_type=F32)


def mm_t(a, b):
    return lax.dot_general(a, b, (((1,), (1,)), ((), ())), preferred_element_type=F32)


def t_mm(a, b):
    return lax.dot_general(a, b, (((0,), (0,)), ((), ())), preferred_element_type=F32)


def norm_parts(rows):
    centre = jnp.mean(rows, axis=-1, keepdims=True)
    spread = jnp.mean(jnp.square(rows - centre), axis=-1, keepdims=True)
    inv = lax.rsqrt(spread + EPS)
    return (rows - centre) * inv, inv


def norm_back(grad, xhat, inv, gain):
    scaled = grad * gain
    return inv * (
        scaled
        - jnp.mean(scaled, axis=-1, keepdims=True)
        - xhat * jnp.mean(scaled * xhat, axis=-1, keepdims=True)
    )


def visible_of(n_rows, n_keys, length, causal):
    cols = lax.broadcasted_iota(jnp.int32, (n_rows, n_keys), 1)
    seen = cols < length
    if causal:
        seen = seen & (cols <= lax.broadcasted_iota(jnp.int32, (n_rows, n_keys), 0))
    return seen


def attend(q, k, v, length, causal):
    factor = HEAD_DIM ** (-0.5)
    seen = visible_of(q.shape[0], k.shape[0], length, causal)
    outs, sums = [], []
    for at in range(0, q.shape[1], HEAD_DIM):
        cols = slice(at, at + HEAD_DIM)
        score = jnp.where(seen, mm_t(q[:, cols], k[:, cols]) * factor, NEGATIVE)
        top = jnp.max(score, axis=1, keepdims=True)
        raised = jnp.exp(score - top)
        total = jnp.sum(raised, axis=1, keepdims=True)
        outs.append(mm((raised / total).astype(BF), v[:, cols]))
        sums.append(top + jnp.log(total))
    return jnp.concatenate(outs, axis=1).astype(BF), jnp.concatenate(sums, axis=1)


def attend_back(q, k, v, dctx, lse, length, causal):
    factor = HEAD_DIM ** (-0.5)
    seen = visible_of(q.shape[0], k.shape[0], length, causal)
    dqs, dks, dvs = [], [], []
    for head, at in enumerate(range(0, q.shape[1], HEAD_DIM)):
        cols = slice(at, at + HEAD_DIM)
        score = mm_t(q[:, cols], k[:, cols]) * factor
        probs = jnp.where(seen, jnp.exp(score - lse[:, head : head + 1]), 0.0)
        dprobs = mm_t(dctx[:, cols], v[:, cols])
        inner = jnp.sum(probs * dprobs, axis=1, keepdims=True)
        dscore = (probs * (dprobs - inner)).astype(BF)
        dqs.append(mm(dscore, k[:, cols]) * factor)
        dks.append(t_mm(dscore, q[:, cols]) * factor)
        dvs.append(t_mm(probs.astype(BF), dctx[:, cols]))
    return tuple(jnp.concatenate(part, axis=1).astype(BF) for part in (dqs, dks, dvs))


def gather_rows(block):
    return lax.all_gather(block, "sp", axis=0, tiled=True)


def gather_cols(block):
    return lax.all_gather(block, "sp", axis=1, tiled=True)


def scatter_rows(part):
    return lax.psum_scatter(part.astype(BF), "sp", scatter_dimension=0, tiled=True).astype(F32)


def gelu_parts(u):
    phi = 0.5 * (1.0 + lax.erf(u * (2.0**-0.5)))
    slope = phi + u * jnp.exp(-0.5 * u * u) * ((2.0 * jnp.pi) ** -0.5)
    return u * phi, slope


def on_device(n_dp, n_sp, *arrays):
    (
        frames, text, frame_len, text_len, cotangent,
        w_q, w_k, w_v, w_o, c_q, c_k, c_v, c_o, f_up, f_down,
        gain_a, bias_a, gain_c, bias_c, gain_f, bias_f,
    ) = arrays
    clips, local, width = frames.shape
    assert clips == 1
    rank = lax.axis_index("sp")
    own = width // n_sp
    block = w_q.shape[0]
    hidden = f_up.shape[1]
    unit = f_down.shape[0] // n_sp
    flen, tlen = frame_len[0], text_len[0]

    def own_cols(weight):
        return lax.dynamic_slice_in_dim(weight, rank * own, own, axis=1)

    def own_rows(rows):
        return lax.dynamic_slice_in_dim(rows, rank * local, local, axis=0)

    def from_dp(part):
        return lax.all_gather(part, "dp", axis=0, tiled=True)

    small = jnp.stack([gain_a, bias_a, gain_c, bias_c, gain_f, bias_f], axis=1)
    small = jnp.pad(small, ((0, 0), (0, 128 - small.shape[1])))
    first = from_dp(jnp.concatenate([own_cols(w) for w in (w_q, w_k, w_v)] + [small], axis=1))
    second = from_dp(jnp.concatenate([own_cols(w) for w in (w_o, c_q, c_o, c_k, c_v)], axis=1))
    up_own = lax.dynamic_slice_in_dim(
        f_up.reshape(block, n_dp, n_sp, unit), rank, 1, axis=2
    ).reshape(block, n_dp * unit)
    up = from_dp(up_own)
    down = from_dp(lax.dynamic_slice_in_dim(f_down, rank * unit, unit, axis=0))

    qkv_w = first[:, : 3 * own]
    vecs = first[:, 3 * own : 3 * own + 6].astype(F32).T
    ga, ba, gc, bc, gf, bf = (vecs[i : i + 1] for i in range(6))
    full3 = lax.all_gather(second[:, : 3 * own], "sp", axis=0, tiled=False)
    o_full, cq_full, co_full = (
        jnp.transpose(full3[:, :, i * own : (i + 1) * own], (1, 0, 2)).reshape(width, width)
        for i in range(3)
    )
    cq_own = second[:, own : 2 * own]
    ckv_own = second[:, 3 * own :]

    x = gather_rows(frames[0]).astype(F32)
    cot = gather_rows(cotangent[0])
    txt = gather_rows(text[0])

    hat1, _ = norm_parts(x)
    h1 = (hat1 * ga + ba).astype(BF)
    qkv = mm(h1, qkv_w).astype(BF)
    q, k, v = (qkv[:, i * own : (i + 1) * own] for i in range(3))
    ctx_own, lse = attend(q, k, v, flen, True)
    ctx = gather_cols(ctx_own)
    mid = x + mm(ctx, o_full)
    hat2, inv2 = norm_parts(mid)
    h2 = (hat2 * gc + bc).astype(BF)
    q2 = mm(h2, cq_own).astype(BF)
    kv2 = mm(txt, ckv_own).astype(BF)
    k2, v2 = kv2[:, :own], kv2[:, own:]
    ctx2_own, lse2 = attend(q2, k2, v2, tlen, False)
    ctx2 = gather_cols(ctx2_own)
    after = mid + mm(ctx2, co_full)
    hat3, _ = norm_parts(after)
    h3 = (hat3 * gf + bf).astype(BF)
    u = mm(h3, up)
    act, slope = gelu_parts(u)
    act = act.astype(BF)
    after_own = own_rows(after)
    output = (after_own + scatter_rows(mm(act, down))).astype(BF).reshape(frames.shape)

    du = (mm_t(cot, down) * slope).astype(BF)
    part_down = t_mm(act, cot).astype(BF).reshape(n_dp * block, unit * width // block)
    part_ffn = jnp.concatenate([part_down, t_mm(h3, du).astype(BF)], axis=1)
    sum_ffn = lax.psum_scatter(part_ffn, "dp", scatter_dimension=0, tiled=True)
    e3 = scatter_rows(mm_t(du, up))
    hat, inv = norm_parts(after_own)
    d_after_own = cotangent[0].astype(F32) + norm_back(e3, hat, inv, gf)
    sums = [jnp.sum(e3 * hat, axis=0), jnp.sum(e3, axis=0)]
    da2 = gather_rows(d_after_own.astype(BF))
    dctx2 = mm_t(da2, lax.dynamic_slice_in_dim(co_full, rank * own, own, axis=0)).astype(BF)
    dq2, dk2, dv2 = attend_back(q2, k2, v2, dctx2, lse2, tlen, False)
    dq2_full = gather_cols(dq2)
    part_cross = jnp.concatenate(
        [t_mm(ctx2, own_cols(da2)), t_mm(h2, dq2), t_mm(txt, jnp.concatenate([dk2, dv2], axis=1))],
        axis=1,
    ).astype(BF)
    sum_cross = lax.psum_scatter(part_cross, "dp", scatter_dimension=0, tiled=True)
    grad_text = scatter_rows(mm_t(jnp.concatenate([dk2, dv2], axis=1), ckv_own))
    e2 = mm_t(dq2_full, cq_full)
    back2 = norm_back(e2, hat2, inv2, gc)
    da = (da2.astype(F32) + back2).astype(BF)
    e2_own = own_rows(e2)
    hat2_own = own_rows(hat2)
    d_mid_own = d_after_own + own_rows(back2)
    sums = [jnp.sum(e2_own * hat2_own, axis=0), jnp.sum(e2_own, axis=0)] + sums
    dctx = mm_t(da, lax.dynamic_slice_in_dim(o_full, rank * own, own, axis=0)).astype(BF)
    dq, dk, dv = attend_back(q, k, v, dctx, lse, flen, True)
    dqkv = jnp.concatenate([dq, dk, dv], axis=1)
    e1 = scatter_rows(mm_t(dqkv, qkv_w))
    hat, inv = norm_parts(frames[0].astype(F32))
    grad_frames = (d_mid_own + norm_back(e1, hat, inv, ga)).reshape(frames.shape)
    sums = [jnp.sum(e1 * hat, axis=0), jnp.sum(e1, axis=0)] + sums
    sums = jnp.pad(jnp.stack(sums, axis=1), ((0, 0), (0, 122)))
    part_self = jnp.concatenate(
        [t_mm(ctx, own_cols(da)), t_mm(h1, dqkv), sums], axis=1
    ).astype(BF)
    sum_self = lax.psum_scatter(part_self, "dp", scatter_dimension=0, tiled=True)

    done = lax.all_gather(
        jnp.concatenate([sum_ffn, sum_cross, sum_self], axis=1), "sp", axis=0, tiled=False
    ).astype(F32)
    at = unit * width // block
    grad_down = done[:, :, :at].reshape(n_sp * unit, width)
    grad_up = done[:, :, at : at + n_dp * unit].reshape(n_sp, block, n_dp, unit)
    grad_up = jnp.transpose(grad_up, (1, 2, 0, 3)).reshape(block, hidden)
    at += n_dp * unit
    squares = []
    for _ in range(8):
        squares.append(jnp.transpose(done[:, :, at : at + own], (1, 0, 2)).reshape(block, width))
        at += own
    g_co, g_cq, g_ck, g_cv, g_o, g_q, g_k, g_v = squares
    vec = jnp.sum(done[:, :, at : at + 6], axis=0)
    return (
        output, grad_frames, grad_text.reshape(text.shape),
        g_q, g_k, g_v, g_o, g_cq, g_ck, g_cv, g_co, grad_up, grad_down,
    ) + tuple(vec[:, i] for i in range(6))


def solution(mesh):
    rows, flat, vec = P("dp", "sp", None), P("dp", None), P("dp")
    return jax.shard_map(
        partial(on_device, mesh.shape["dp"], mesh.shape["sp"]),
        mesh=mesh,
        in_specs=(rows, rows, vec, vec, rows) + (flat,) * 10 + (vec,) * 6,
        out_specs=(rows, rows, rows) + (flat,) * 10 + (vec,) * 6,
        check_vma=False,
    )
```

time: 1730 us -> 1030 us (0.60)
  waiting for transfers between devices: 940 us -> 643 us
  blocking collectives: 206 us -> 10.5 us
  other arithmetic: 146 us -> 72.2 us
  local copies, waits for them, and re-layouts: 154 us -> 94.4 us
  starting transfers between devices: 44.8 us -> 2.27 us
  matrix products: 205 us -> 181 us
    reduce_scatter x8 -> x4, waiting for transfers between devices: 566 us -> 79 us  [scatter_rows(): lax.psum_scatter(part.astype(BF), 'sp', scatter_dimension=0, tiled=True)]
    unnamed x23 -> x22, waiting for transfers between devices: 5.93 us -> 212 us
    all_gather x6 -> x1, blocking collectives: 110 us -> 10.5 us  [gather_rows(): return lax.all_gather(block, 'sp', axis=0, tiled=True)]
    unnamed x22 -> x6, other arithmetic: 90.1 us -> 0.01 us
    unnamed x394 -> x248, local copies, waits for them, and re-layouts: 101 us -> 40.1 us
    all_to_all x5 -> x0, blocking collectives: 55.5 us -> none  [the longest x1 14.4 us: on_device(): lax.all_to_all(as_sent(grad_hk), 'sp', split_axis=1, concat_axis=2, tiled...]
    all_to_all x11 -> x0, starting transfers between devices: 41.9 us -> none  [the longest x3 10.6 us: to_heads(): return lax.all_to_all(block, 'sp', split_axis=2, concat_axis=1, tiled=True)]
    all_gather x10 -> x12, waiting for transfers between devices: 311 us -> 352 us  [the longest x4 183 us: from_dp(): return lax.all_gather(part, 'dp', axis=0, tiled=True)]
  transfers between devices with their start and end apart: 32 -> 19, of which waited for: 17 -> 18; matrix products, arithmetic and copies ran while one was open for 24% -> 15% of each run, Pallas kernels for 0% -> 0%
where the time goes in v1:
time: 1030 us; the launch traced here: 1020 us
  waiting for transfers between devices  643 us (62%)
  matrix products  181 us (18%)
  local copies, waits for them, and re-layouts  94.4 us (9%)
  other arithmetic  72.2 us (7%)
  between operations  17.7 us (2%)
  blocking collectives  10.5 us (1%)
    unnamed x22, waiting for transfers between devices  212 us
    all_gather x4, waiting for transfers between devices, from_dp(): return lax.all_gather(part, 'dp', axis=0, tiled=True)  183 us
    reduce_scatter x4, waiting for transfers between devices, scatter_rows(): lax.psum_scatter(part.astype(BF), 'sp', scatter_dimension=0, tiled=True)  79 us
    dot_general x23, matrix products, mm_t(): lax.dot_general(a, b, (((1,), (1,)), ((), ())), preferred_element_type=F32)  76.4 us
    all_gather x3, waiting for transfers between devices, gather_rows(): return lax.all_gather(block, 'sp', axis=0, tiled=True)  74.5 us
    all_gather x3, waiting for transfers between devices, gather_cols(): return lax.all_gather(block, 'sp', axis=1, tiled=True)  56.8 us
    dot_general x23, matrix products, mm(): return jnp.dot(a, b, preferred_element_type=F32)  55.3 us
    dot_general x23, matrix products, t_mm(): lax.dot_general(a, b, (((0,), (0,)), ((), ())), preferred_element_type=F32)  49.5 us
  transfers between devices with their start and end apart: 19, of which 18 were waited for; matrix products, arithmetic and copies ran while one was open for 15% of the time, Pallas kernels for 0%

profile of v1, /device:TPU:0, one launch (start us, length us, event | category | flops | bytes accessed | tf_op | source)
XLA Modules:
  0.0 1021.3 jit_solution(4110626244872414495)
XLA Ops:
  17.2 42.8 %all-gather.18.cloned.1.call-done = bf16[1024,896]{1,0:T(8,128)(2,1)} async-done(((bf16[128,896]{1,0:T(8,128)(2,1)}), bf16[1024,896]{1,0:T(8,128)(2,1)}) %all-gather.18.cloned.1.call-update) | async-done | bytes 1835024 | tf_op jit(solution)/shard_map/all_gather | solution.py:123
  62.6 23.2 %all-gather.34.cloned.1.call-done = bf16[1,1280,1024]{2,1,0:T(8,128)(2,1)} async-done(((bf16[1,320,1024]{2,1,0:T(8,128)(2,1)}), bf16[1,1280,1024]{2,1,0:T(8,128)(2,1)}) %all-gather.34.cloned.1.call-update) | async-done | bytes 2621456 | tf_op jit(solution)/shard_map/all_gather | solution.py:84
  88.0 55.0 %all-gather.22.cloned.1.call-done = bf16[1024,1280]{1,0:T(8,128)(2,1)} async-done(((bf16[128,1280]{1,0:T(8,128)(2,1)}), bf16[1024,1280]{1,0:T(8,128)(2,1)}) %all-gather.22.cloned.1.call-update) | async-done | bytes 2621456 | tf_op jit(solution)/shard_map/all_gather | solution.py:123
  160.0 5.9 fusion.10
  176.2 10.5 %all-gather.2 = bf16[1,256,1024]{2,1,0:T(8,128)(2,1)S(1)} all-gather(bf16[1,64,1024]{2,1,0:T(8,128)(2,1)S(1)} %copy-done.53), channel_id=4, replica_groups=mesh['dp'=8,'sp'=4] {'sp'}, dimensions={1}, use_global_device_ids=true | all-gather | bytes 655360 | tf_op jit(solution)/shard_map/all_gather | solution.py:84
  193.7 5.3 slice_bitcast_fusion
  201.5 19.8 %all-gather.20.cloned.1.call-done = bf16[1280,1024]{0,1:T(8,128)(2,1)} async-done(((bf16[1280,256]{0,1:T(8,128)(2,1)}), bf16[1280,1024]{0,1:T(8,128)(2,1)}) %all-gather.20.cloned.1.call-update) | async-done | bytes 2621456 | tf_op jit(solution)/shard_map/all_gather | solution.py:88
  221.3 6.3 fusion.263
  248.3 15.9 %all-gather.24.cloned.1.call-done = bf16[1280,1024]{0,1:T(8,128)(2,1)} async-done(((bf16[1280,256]{0,1:T(8,128)(2,1)}), bf16[1280,1024]{0,1:T(8,128)(2,1)}) %all-gather.24.cloned.1.call-update) | async-done | bytes 2621456 | tf_op jit(solution)/shard_map/all_gather | solution.py:88
  264.2 7.1 fusion.264
  273.6 43.6 %all-gather.26.cloned.1.call-done = bf16[1024,1024]{0,1:T(8,128)(2,1)} async-done(((bf16[128,1024]{0,1:T(8,128)(2,1)}), bf16[1024,1024]{0,1:T(8,128)(2,1)}) %all-gather.26.cloned.1.call-update) | async-done | bytes 2097168 | tf_op jit(solution)/shard_map/all_gather | solution.py:123
  317.2 8.1 multiply_convert_fusion.4
  325.3 41.9 %all-gather.28.cloned.1.call-done = bf16[1024,1024]{1,0:T(8,128)(2,1)} async-done(((bf16[128,1024]{1,0:T(8,128)(2,1)}), bf16[1024,1024]{1,0:T(8,128)(2,1)}) %all-gather.28.cloned.1.call-update) | async-done | bytes 2097168 | tf_op jit(solution)/shard_map/all_gather | solution.py:123
  367.2 25.7 %all-gather.38.cloned.1.call-done = bf16[1,1280,1024]{2,1,0:T(8,128)(2,1)} async-done(((bf16[1,320,1024]{2,1,0:T(8,128)(2,1)}), bf16[1,1280,1024]{2,1,0:T(8,128)(2,1)}) %all-gather.38.cloned.1.call-update) | async-done | bytes 2621456 | tf_op jit(solution)/shard_map/all_gather | solution.py:84
  392.9 7.6 fusion.22
  406.3 6.8 convolution_convert_fusion.2
  416.8 24.1 %reduce-scatter.16.cloned.1.call-done = bf16[320,1024]{1,0:T(8,128)(2,1)} async-done(((bf16[1280,1024]{1,0:T(8,128)(2,1)}), bf16[320,1024]{1,0:T(8,128)(2,1)}) %reduce-scatter.16.cloned.1.call-update) | async-done | bytes 655376 | tf_op jit(solution)/shard_map/reduce_scatter | solution.py:92
  443.7 34.3 %reduce-scatter.14.cloned.1.call-done = bf16[320,1024]{1,0:T(8,128)(2,1)} async-done(((bf16[1280,1024]{1,0:T(8,128)(2,1)}), bf16[320,1024]{1,0:T(8,128)(2,1)}) %reduce-scatter.14.cloned.1.call-update) | async-done | bytes 655376 | tf_op jit(solution)/shard_map/reduce_scatter | solution.py:92
  482.0 25.6 %all-gather.30.cloned.1.call-done = bf16[1280,1024]{1,0:T(8,128)(2,1)} async-done(((bf16[320,1024]{1,0:T(8,128)(2,1)}), bf16[1280,1024]{1,0:T(8,128)(2,1)}) %all-gather.30.cloned.1.call-update) | async-done | bytes 2621456 | tf_op jit(solution)/shard_map/all_gather | solution.py:84
  522.6 21.1 %all-gather.32.cloned.1.call-done = bf16[1280,1024]{0,1:T(8,128)(2,1)} async-done(((bf16[1280,256]{0,1:T(8,128)(2,1)}), bf16[1280,1024]{0,1:T(8,128)(2,1)}) %all-gather.32.cloned.1.call-update) | async-done | bytes 2621456 | tf_op jit(solution)/shard_map/all_gather | solution.py:88
  543.8 7.7 multiply_reduce_fusion.7
  571.9 19.4 %multiply_reduce_fusion = (f32[1280]{0:T(1024)S(1)}, f32[1280]{0:T(1024)S(1)}, f32[1280]{0:T(1024)S(1)}, f32[1280]{0:T(1024)S(1)}, f32[1280,1280]{0,1:T(8,128)}) fusion(f32[1280,1280]{0,1:T(8,128)} %copy-done.4, f32[1280]{0:T(1024)S(1)} %log_add_fusion, pred[1280]{0:T(1024)(128)(4,1)S(1)} %copy-done.59, f32[1280,1280]{0,1:T(8,128)} %fusion.173, ...), kind=kOutput, calls=%fused_computation.6 | convolution fusion | flops 239201280 | bytes 52798720 | tf_op jit(solution)/shard_map/dot_general | solution.py:20
  591.3 21.8 %multiply_convert_fusion = (bf16[1280,1280]{0,1:T(8,128)(2,1)S(1)}, bf16[1280,1280]{0,1:T(8,128)(2,1)S(1)}, bf16[1280,1280]{0,1:T(8,128)(2,1)}, bf16[1280,1280]{0,1:T(8,128)(2,1)}) fusion(f32[1280,1280]{0,1:T(8,128)} %get-tuple-element.103, f32[1280]{0:T(1024)S(1)} %get-tuple-element.35, f32[1280,1280]{0,1:T(8,128)} %copy-done.4, f32[1280]{0:T(1024)S(1)} %log_add_fusion, ...), kind=kLoop, calls=%fused_computation.5 | loop fusion | flops 36044800 | bytes 65578240 | tf_op jit(solution)/shard_map/convert_element_type | solution.py:76
  646.4 5.6 fusion.92
  652.0 6.4 convolution_convert_fusion.11
  660.8 6.5 copy.97
  703.6 69.1 %reduce-scatter.22.cloned.1.call-done = bf16[128,2048]{1,0:T(8,128)(2,1)} async-done(((bf16[1024,2048]{1,0:T(8,128)(2,1)}), bf16[128,2048]{1,0:T(8,128)(2,1)}) %reduce-scatter.22.cloned.1.call-update) | async-done | bytes 524304
  774.1 70.7 %reduce-scatter.24.cloned.1.call-done = bf16[128,1024]{1,0:T(8,128)(2,1)} async-done(((bf16[1024,1024]{1,0:T(8,128)(2,1)}), bf16[128,1024]{1,0:T(8,128)(2,1)}) %reduce-scatter.24.cloned.1.call-update) | async-done | bytes 262160
  846.5 70.2 %reduce-scatter.26.cloned.1.call-done = bf16[128,1152]{1,0:T(8,128)(2,1)} async-done(((bf16[1024,1152]{1,0:T(8,128)(2,1)}), bf16[128,1152]{1,0:T(8,128)(2,1)}) %reduce-scatter.26.cloned.1.call-update) | async-done | bytes 294928
  920.0 20.6 %reduce-scatter.20.cloned.1.call-done = bf16[64,1024]{1,0:T(8,128)(2,1)} async-done(((bf16[256,1024]{1,0:T(8,128)(2,1)}), bf16[64,1024]{1,0:T(8,128)(2,1)}) %reduce-scatter.20.cloned.1.call-update) | async-done | bytes 131088 | tf_op jit(solution)/shard_map/reduce_scatter | solution.py:92
  945.1 33.4 %all-gather.40.cloned.1.call-done = bf16[512,4224]{0,1:T(8,128)(2,1)} async-done(((bf16[128,4224]{0,1:T(8,128)(2,1)}), bf16[512,4224]{0,1:T(8,128)(2,1)}) %all-gather.40.cloned.1.call-update) | async-done | bytes 4325392 | tf_op jit(solution)/shard_map/all_gather | solution.py:211
  978.5 9.1 reshape.300
  (441 shorter events, 232.6 us)
Async XLA Ops:
  7.2 235.4 %copy-start = (bf16[512,1024]{1,0:T(8,128)(2,1)S(1)}, bf16[512,1024]{1,0:T(8,128)(2,1)}, u32[]{:S(2)}) copy-start(bf16[512,1024]{1,0:T(8,128)(2,1)} %param.35) | copy-start | bytes 3145732
  7.2 52.7 %all-gather.18.cloned.1.call-start = ((), (), s32[]{:S(2)}) async-start(), calls=%async_computation.7 | async-start | bytes 2064384 | tf_op jit(solution)/shard_map/all_gather | solution.py:123
  10.7 75.1 %all-gather.34.cloned.1.call-start = ((), (), s32[]{:S(2)}) async-start(), calls=%async_computation.19 | async-start | bytes 3276800 | tf_op jit(solution)/shard_map/all_gather | solution.py:84
  11.5 131.5 %all-gather.22.cloned.1.call-start = ((), (), s32[]{:S(2)}) async-start(), calls=%async_computation.9 | async-start | bytes 2949120 | tf_op jit(solution)/shard_map/all_gather | solution.py:123
  16.5 177.2 %all-gather.36.cloned.1.call-start = ((), (), s32[]{:S(2)}) async-start(), calls=%async_computation.20 | async-start | bytes 7864320 | tf_op jit(solution)/shard_map/all_gather | solution.py:138
  17.2 155.2 %copy-start.58 = (pred[1280]{0:T(1024)(128)(4,1)}, pred[1280]{0:T(1024)(128)(4,1)S(1)}, u32[]{:S(2)}) copy-start(pred[1280]{0:T(1024)(128)(4,1)S(1)} %iota_compare_fusion.3) | copy-start | bytes 3844
  62.5 86.4 %copy-start.56 = (f32[1024]{0:T(1024)}, f32[1024]{0:T(1024)S(1)}, u32[]{:S(2)}) copy-start(f32[1024]{0:T(1024)S(1)} %get-tuple-element.34) | copy-start | bytes 12292
  62.5 86.4 %copy-start.92 = (f32[1024]{0:T(1024)}, f32[1024]{0:T(1024)S(1)}, u32[]{:S(2)}) copy-start(f32[1024]{0:T(1024)S(1)} %get-tuple-element.33) | copy-start | bytes 12292
  62.5 167.8 %copy-start.76 = (f32[1024]{0:T(1024)}, f32[1024]{0:T(1024)S(1)}, u32[]{:S(2)}) copy-start(f32[1024]{0:T(1024)S(1)} %get-tuple-element.32) | copy-start | bytes 12292
  62.6 167.8 %copy-start.94 = (f32[1024]{0:T(1024)}, f32[1024]{0:T(1024)S(1)}, u32[]{:S(2)}) copy-start(f32[1024]{0:T(1024)S(1)} %get-tuple-element.31) | copy-start | bytes 12292
  62.6 254.6 %copy-start.96 = (f32[1024]{0:T(1024)}, f32[1024]{0:T(1024)S(1)}, u32[]{:S(2)}) copy-start(f32[1024]{0:T(1024)S(1)} %get-tuple-element.30) | copy-start | bytes 12292
  88.0 61.0 %copy-start.72 = (f32[1280]{0:T(1024)}, f32[1280]{0:T(1024)S(1)}, u32[]{:S(2)}) copy-start(f32[1280]{0:T(1024)S(1)} %broadcast_multiply_fusion.4) | copy-start | bytes 15364
  145.8 75.5 %all-gather.20.cloned.1.call-start = ((), (), s32[]{:S(2)}) async-start(), calls=%async_computation.8 | async-start | bytes 3276800 | tf_op jit(solution)/shard_map/all_gather | solution.py:88
  175.5 88.7 %all-gather.24.cloned.1.call-start = ((), (), s32[]{:S(2)}) async-start(), calls=%async_computation.10 | async-start | bytes 3276800 | tf_op jit(solution)/shard_map/all_gather | solution.py:88
  176.2 337.8 %copy-start.81 = (pred[256]{0:T(512)(128)(4,1)}, pred[256]{0:T(512)(128)(4,1)S(1)}, u32[]{:S(2)}) copy-start(pred[256]{0:T(512)(128)(4,1)S(1)} %iota_compare_fusion.4) | copy-start | bytes 772
  189.2 322.2 %copy-start.48 = (bf16[256,512]{0,1:T(8,128)(2,1)}, bf16[256,512]{0,1:T(8,128)(2,1)S(1)}, u32[]{:S(2)}) copy-start(bf16[256,512]{0,1:T(8,128)(2,1)S(1)} %fusion.120) | copy-start | bytes 786436
  238.5 78.7 %all-gather.26.cloned.1.call-start = ((), (), s32[]{:S(2)}) async-start(), calls=%async_computation.11 | async-start | bytes 2359296 | tf_op jit(solution)/shard_map/all_gather | solution.py:123
  242.5 124.7 %all-gather.28.cloned.1.call-start = ((), (), s32[]{:S(2)}) async-start(), calls=%async_computation.12 | async-start | bytes 2359296 | tf_op jit(solution)/shard_map/all_gather | solution.py:123
  243.3 149.5 %all-gather.38.cloned.1.call-start = ((), (), s32[]{:S(2)}) async-start(), calls=%async_computation.21 | async-start | bytes 3276800 | tf_op jit(solution)/shard_map/all_gather | solution.py:84
  244.1 196.9 %reduce-scatter.16.cloned.1.call-start = ((), (), s32[]{:S(2)}) async-start(), calls=%async_computation.14 | async-start | bytes 3276800 | tf_op jit(solution)/shard_map/reduce_scatter | solution.py:92
  406.3 71.7 %reduce-scatter.14.cloned.1.call-start = ((), (), s32[]{:S(2)}) async-start(), calls=%async_computation.13 | async-start | bytes 3276800 | tf_op jit(solution)/shard_map/reduce_scatter | solution.py:92
  413.1 64.9 %copy-start.31 = (bf16[1,320,1024]{2,1,0:T(8,128)(2,1)S(1)}, bf16[1,320,1024]{2,1,0:T(8,128)(2,1)}, u32[]{:S(2)}) copy-start(bf16[1,320,1024]{2,1,0:T(8,128)(2,1)} %param.25) | copy-start | bytes 1966084
  413.1 94.4 %all-gather.30.cloned.1.call-start = ((), (), s32[]{:S(2)}) async-start(), calls=%async_computation.15 | async-start | bytes 3276800 | tf_op jit(solution)/shard_map/all_gather | solution.py:84
  481.9 61.9 %all-gather.32.cloned.1.call-start = ((), (), s32[]{:S(2)}) async-start(), calls=%async_computation.16 | async-start | bytes 3276800 | tf_op jit(solution)/shard_map/all_gather | solution.py:88
  518.1 175.4 %reduce-scatter.18.cloned.1.call-start = ((), (), s32[]{:S(2)}) async-start(), calls=%async_computation.17 | async-start | bytes 3276800 | tf_op jit(solution)/shard_map/reduce_scatter | solution.py:92
  646.3 126.5 %reduce-scatter.22.cloned.1.call-start = ((), (), s32[]{:S(2)}) async-start(), calls=%async_computation.23 | async-start | bytes 4718592
  667.4 177.3 %reduce-scatter.24.cloned.1.call-start = ((), (), s32[]{:S(2)}) async-start(), calls=%async_computation.24 | async-start | bytes 2359296
  682.7 234.1 %reduce-scatter.26.cloned.1.call-start = ((), (), s32[]{:S(2)}) async-start(), calls=%async_computation.25 | async-start | bytes 2654208
  700.8 239.7 %reduce-scatter.20.cloned.1.call-start = ((), (), s32[]{:S(2)}) async-start(), calls=%async_computation.18 | async-start | bytes 655360 | tf_op jit(solution)/shard_map/reduce_scatter | solution.py:92
  703.4 275.1 %all-gather.40.cloned.1.call-start = ((), (), s32[]{:S(2)}) async-start(), calls=%async_computation.22 | async-start | bytes 5406720 | tf_op jit(solution)/shard_map/all_gather | solution.py:211
  774.1 168.1 %copy-start.26 = (bf16[320,1024]{1,0:T(8,128)(2,1)S(1)}, bf16[320,1024]{1,0:T(8,128)(2,1)}, u32[]{:S(2)}) copy-start(bf16[320,1024]{1,0:T(8,128)(2,1)} %reduce-scatter.18.cloned.1.call-done) | copy-start | bytes 1966084
  774.1 168.1 %copy-start.28 = (f32[320,1024]{1,0:T(8,128)S(1)}, f32[320,1024]{1,0:T(8,128)}, u32[]{:S(2)}) copy-start(f32[320,1024]{1,0:T(8,128)} %get-tuple-element.60) | copy-start | bytes 3932164
  (101 other events, 574.7 us)
Sparse Core Ops, SparseCore 0:
  10.8 49.0 all-gather.17
  61.5 24.2 all-gather.33
  88.6 54.3 all-gather.21
  145.9 47.7 all-gather.35
  195.7 25.5 all-gather.19
  238.6 25.5 all-gather.23
  266.8 50.3 all-gather.25
  319.9 47.2 all-gather.27
  368.7 24.0 all-gather.37
  406.4 34.4 reduce-scatter.15
  443.5 34.4 reduce-scatter.13
  482.0 25.5 all-gather.29
  518.2 25.5 all-gather.31
  646.4 34.4 reduce-scatter.17
  684.4 88.3 reduce-scatter.21
  776.7 67.9 reduce-scatter.23
  848.1 68.6 reduce-scatter.25
  919.7 20.8 reduce-scatter.19
  942.7 35.7 all-gather.39

commit v2 on v1

v2 whole, which is shorter than its diff:
```python
from functools import partial

import jax
import jax.numpy as jnp
from jax import lax
from jax.experimental import pallas as pl
from jax.experimental.pallas import tpu as pltpu
from jax.sharding import PartitionSpec as P

HEAD_DIM = 64
EPS = 1e-05
NEGATIVE = -1e30
BF = jnp.bfloat16
F32 = jnp.float32


def mm(a, b):
    return jnp.dot(a, b, preferred_element_type=F32)


def mm_t(a, b):
    return lax.dot_general(a, b, (((1,), (1,)), ((), ())), preferred_element_type=F32)


def t_mm(a, b):
    return lax.dot_general(a, b, (((0,), (0,)), ((), ())), preferred_element_type=F32)


def norm_parts(rows):
    centre = jnp.mean(rows, axis=-1, keepdims=True)
    spread = jnp.mean(jnp.square(rows - centre), axis=-1, keepdims=True)
    inv = lax.rsqrt(spread + EPS)
    return (rows - centre) * inv, inv


def norm_back(grad, xhat, inv, gain):
    scaled = grad * gain
    return inv * (
        scaled
        - jnp.mean(scaled, axis=-1, keepdims=True)
        - xhat * jnp.mean(scaled * xhat, axis=-1, keepdims=True)
    )


def dot_nt(a, b):
    return lax.dot_general(a, b, (((1,), (1,)), ((), ())), preferred_element_type=F32)


def key_bias(length, n_keys, n_queries, causal):
    rows = lax.broadcasted_iota(jnp.int32, (n_keys, 1), 0)
    bias = jnp.where(rows < length, 0.0, NEGATIVE)
    if not causal:
        return bias, None
    key = lax.broadcasted_iota(jnp.int32, (n_queries, n_queries), 0)
    query = lax.broadcasted_iota(jnp.int32, (n_queries, n_queries), 1)
    return bias, jnp.where(key <= query, 0.0, NEGATIVE)


def scores_t(keys, queries, bias, corner):
    scores = dot_nt(keys, queries)
    if corner is None:
        return scores + bias
    n = corner.shape[0]
    low = scores[-n:] + (bias[-n:] + corner)
    if keys.shape[0] == n:
        return low
    return jnp.concatenate([scores[:-n] + bias[:-n], low], axis=0)


def attend_kernel(causal, step, length_ref, q_ref, k_ref, v_ref, ctx_ref, lse_ref, vt, ctxt):
    heads = q_ref.shape[1] // HEAD_DIM
    n_rows, n_keys = q_ref.shape[0], k_ref.shape[0]
    vt[...] = v_ref[...].T
    lane = lax.broadcasted_iota(jnp.int32, (1, q_ref.shape[1]), 1) // HEAD_DIM
    bias, corner = key_bias(length_ref[0], n_keys, step, causal)

    def one_head(head, carry):
        mask = jnp.where(lane == head, HEAD_DIM**-0.5, 0.0).astype(BF)
        dims = pl.ds(pl.multiple_of(head * HEAD_DIM, HEAD_DIM), HEAD_DIM)
        for at in range(0, n_rows, step):
            seen = at + step if causal else n_keys
            queries = q_ref[at : at + step, :] * mask
            scores = scores_t(k_ref[:seen, :], queries, bias[:seen], corner)
            top = jnp.max(scores, axis=0, keepdims=True)
            raised = jnp.exp(scores - top)
            total = jnp.sum(raised, axis=0, keepdims=True)
            mixed = jnp.dot(vt[dims, :seen], raised.astype(BF), preferred_element_type=F32)
            ctxt[dims, at : at + step] = mixed / total
            lse_ref[pl.ds(head, 1), at : at + step] = top + jnp.log(total)
        return carry

    lax.fori_loop(0, heads, one_head, 0)
    ctx_ref[...] = ctxt[...].T.astype(BF)


def attend_back_kernel(
    causal, step, length_ref, q_ref, k_ref, v_ref, d_ref, lse_ref, dq_ref, dk_ref, dv_ref,
    kt, dqt, dk_sum, dv_sum,
):
    heads = q_ref.shape[1] // HEAD_DIM
    n_rows, n_keys = q_ref.shape[0], k_ref.shape[0]
    kt[...] = k_ref[...].T
    dk_sum[...] = jnp.zeros_like(dk_sum)
    dv_sum[...] = jnp.zeros_like(dv_sum)
    lane = lax.broadcasted_iota(jnp.int32, (1, q_ref.shape[1]), 1) // HEAD_DIM
    bias, corner = key_bias(length_ref[0], n_keys, step, causal)

    def one_head(head, carry):
        mask = jnp.where(lane == head, HEAD_DIM**-0.5, 0.0).astype(BF)
        plain = jnp.where(lane == head, 1.0, 0.0).astype(BF)
        dims = pl.ds(pl.multiple_of(head * HEAD_DIM, HEAD_DIM), HEAD_DIM)
        for at in range(0, n_rows, step):
            seen = at + step if causal else n_keys
            queries = q_ref[at : at + step, :] * mask
            grads = d_ref[at : at + step, :] * plain
            scores = scores_t(k_ref[:seen, :], queries, bias[:seen], corner)
            probs = jnp.exp(scores - lse_ref[pl.ds(head, 1), at : at + step])
            dprobs = dot_nt(v_ref[:seen, :], grads)
            inner = jnp.sum(probs * dprobs, axis=0, keepdims=True)
            dscores = (probs * (dprobs - inner)).astype(BF)
            dqt[dims, at : at + step] = jnp.dot(
                kt[dims, :seen], dscores, preferred_element_type=F32
            ) * (HEAD_DIM**-0.5)
            dk_sum[:seen, :] += jnp.dot(dscores, queries, preferred_element_type=F32)
            dv_sum[:seen, :] += jnp.dot(probs.astype(BF), grads, preferred_element_type=F32)
        return carry

    lax.fori_loop(0, heads, one_head, 0)
    dq_ref[...] = dqt[...].T.astype(BF)
    dk_ref[...] = dk_sum[...].astype(BF)
    dv_ref[...] = dv_sum[...].astype(BF)


STEP = 256
VMEM = pl.BlockSpec(memory_space=pltpu.VMEM)
SMEM = pl.BlockSpec(memory_space=pltpu.SMEM)
LIMIT = 60 * 2**20


def lse_rows(q):
    return max(8, q.shape[1] // HEAD_DIM)


def attend(q, k, v, length, causal):
    n_rows, own = q.shape
    n_keys = k.shape[0]
    work = n_rows * n_keys * own
    return pl.pallas_call(
        partial(attend_kernel, causal, STEP),
        out_shape=(
            jax.ShapeDtypeStruct((n_rows, own), BF),
            jax.ShapeDtypeStruct((lse_rows(q), n_rows), F32),
        ),
        in_specs=[SMEM, VMEM, VMEM, VMEM],
        out_specs=(VMEM, VMEM),
        scratch_shapes=[pltpu.VMEM((own, n_keys), BF), pltpu.VMEM((own, n_rows), F32)],
        compiler_params=pltpu.CompilerParams(vmem_limit_bytes=LIMIT),
        cost_estimate=pl.CostEstimate(
            flops=8 * work, bytes_accessed=4 * q.size * 2, transcendentals=work // HEAD_DIM
        ),
        name="attend",
    )(length, q, k, v)


def attend_back(q, k, v, dctx, lse, length, causal):
    n_rows, own = q.shape
    n_keys = k.shape[0]
    work = n_rows * n_keys * own
    return pl.pallas_call(
        partial(attend_back_kernel, causal, STEP),
        out_shape=(
            jax.ShapeDtypeStruct((n_rows, own), BF),
            jax.ShapeDtypeStruct((n_keys, own), BF),
            jax.ShapeDtypeStruct((n_keys, own), BF),
        ),
        in_specs=[SMEM] + [VMEM] * 5,
        out_specs=(VMEM, VMEM, VMEM),
        scratch_shapes=[
            pltpu.VMEM((own, n_keys), BF),
            pltpu.VMEM((own, n_rows), F32),
            pltpu.VMEM((n_keys, own), F32),
            pltpu.VMEM((n_keys, own), F32),
        ],
        compiler_params=pltpu.CompilerParams(vmem_limit_bytes=LIMIT),
        cost_estimate=pl.CostEstimate(
            flops=20 * work, bytes_accessed=7 * q.size * 2, transcendentals=work // HEAD_DIM
        ),
        name="attend_back",
    )(length, q, k, v, dctx, lse)


def sp_place(n_sp):
    me = lax.axis_index("sp")
    side = lax.rem(me, 2)
    return me, me // 2, side, me + 1 - 2 * side, n_sp // 2


def sp_barrier(n_sp):
    me, y, side, partner, n_y = sp_place(n_sp)
    barrier = pltpu.get_barrier_semaphore()
    pl.semaphore_signal(barrier, inc=1, device_id={"sp": partner})
    for far in range(1, n_y):
        peer = lax.rem(y + far, n_y) * 2 + side
        pl.semaphore_signal(barrier, inc=1, device_id={"sp": peer})
    pl.semaphore_wait(barrier, n_y)


def remote(src, dst, send, recv, peer):
    return pltpu.make_async_remote_copy(
        src_ref=src, dst_ref=dst, send_sem=send, recv_sem=recv, device_id={"sp": peer}
    )


def gather_kernel(n_sp, axes, *refs):
    count = len(axes)
    ins, outs = refs[:count], refs[count : 2 * count]
    send, recv = refs[2 * count :]
    me, y, side, partner, n_y = sp_place(n_sp)

    def spot(which, owner):
        size = ins[which].shape[axes[which]]
        span = pl.ds(pl.multiple_of(owner * size, size), size)
        return outs[which].at[span] if axes[which] == 0 else outs[which].at[:, span]

    sp_barrier(n_sp)
    copies = []
    for which in range(count):
        for far in range(1, n_y):
            peer = lax.rem(y + far, n_y) * 2 + side
            copies.append(
                remote(ins[which], spot(which, me), send.at[which, far], recv.at[which, far], peer)
            )
            copies[-1].start()
        copies.append(
            remote(ins[which], spot(which, me), send.at[which, 0], recv.at[which, 0], partner)
        )
        copies[-1].start()
    for which in range(count):
        spot(which, me)[...] = ins[which][...]
    relays = []
    for which in range(count):
        for far in range(1, n_y):
            copies[which * n_y + far - 1].wait_recv()
            origin = lax.rem(y + n_y - far, n_y) * 2 + side
            at = spot(which, origin)
            slot = n_y - 1 + far
            relays.append(remote(at, at, send.at[which, slot], recv.at[which, slot], partner))
            relays[-1].start()
    for which in range(count):
        for far in range(1, n_y):
            copies[which * n_y + far - 1].wait_send()
        copies[which * n_y + n_y - 1].wait()
    for copy in relays:
        copy.wait()


def sp_gather(n_sp, ident, blocks, axes):
    shapes = []
    for block, axis in zip(blocks, axes):
        shape = list(block.shape)
        shape[axis] *= n_sp
        shapes.append(jax.ShapeDtypeStruct(tuple(shape), block.dtype))
    sent = sum(block.size * block.dtype.itemsize for block in blocks) * n_sp
    return pl.pallas_call(
        partial(gather_kernel, n_sp, axes),
        out_shape=tuple(shapes),
        in_specs=[VMEM] * len(blocks),
        out_specs=(VMEM,) * len(blocks),
        scratch_shapes=[
            pltpu.SemaphoreType.DMA((len(blocks), n_sp)),
            pltpu.SemaphoreType.DMA((len(blocks), n_sp)),
        ],
        compiler_params=pltpu.CompilerParams(
            collective_id=ident, has_side_effects=True, vmem_limit_bytes=LIMIT
        ),
        cost_estimate=pl.CostEstimate(flops=0, bytes_accessed=20 * sent, transcendentals=0),
        name="sp_gather",
    )(*blocks)


def scatter_kernel(n_sp, part_ref, out_ref, near, chip, far_in, send, recv):
    me, y, side, partner, n_y = sp_place(n_sp)
    size = out_ref.shape[0]

    def mine(owner):
        return part_ref.at[pl.ds(pl.multiple_of(owner * size, size), size)]

    sp_barrier(n_sp)
    firsts, seconds = [], []
    for far in range(1, n_y + 1):
        row = lax.rem(y + far, n_y)
        slot = far % n_y
        firsts.append(
            remote(mine(row * 2 + 1 - side), near.at[slot], send.at[slot], recv.at[slot], partner)
        )
        firsts[-1].start()
    for far in range(1, n_y):
        peer = lax.rem(y + far, n_y) * 2 + side
        firsts[far - 1].wait_recv()
        chip[far] = (mine(peer)[...].astype(F32) + near[far].astype(F32)).astype(BF)
        slot = n_y - 1 + far
        seconds.append(remote(chip.at[far], far_in.at[far], send.at[slot], recv.at[slot], peer))
        seconds[-1].start()
    firsts[n_y - 1].wait_recv()
    out_ref[...] = mine(me)[...].astype(F32) + near[0].astype(F32)
    for far in range(1, n_y):
        seconds[far - 1].wait_recv()
        out_ref[...] += far_in[far].astype(F32)
    for copy in firsts + seconds:
        copy.wait_send()


def sp_scatter(n_sp, ident, part):
    rows, width = part.shape
    size, n_y = rows // n_sp, n_sp // 2
    room = pltpu.VMEM((n_y, size, width), BF)
    return pl.pallas_call(
        partial(scatter_kernel, n_sp),
        out_shape=jax.ShapeDtypeStruct((size, width), F32),
        in_specs=[VMEM],
        out_specs=VMEM,
        scratch_shapes=[room, room, room]
        + [pltpu.SemaphoreType.DMA((n_sp,)), pltpu.SemaphoreType.DMA((n_sp,))],
        compiler_params=pltpu.CompilerParams(
            collective_id=ident, has_side_effects=True, vmem_limit_bytes=LIMIT
        ),
        cost_estimate=pl.CostEstimate(flops=0, bytes_accessed=40 * part.size, transcendentals=0),
        name="sp_scatter",
    )(part.astype(BF))


def gelu_parts(u):
    phi = 0.5 * (1.0 + lax.erf(u * (2.0**-0.5)))
    slope = phi + u * jnp.exp(-0.5 * u * u) * ((2.0 * jnp.pi) ** -0.5)
    return u * phi, slope


def on_device(n_dp, n_sp, *arrays):
    (
        frames, text, frame_len, text_len, cotangent,
        w_q, w_k, w_v, w_o, c_q, c_k, c_v, c_o, f_up, f_down,
        gain_a, bias_a, gain_c, bias_c, gain_f, bias_f,
    ) = arrays
    clips, local, width = frames.shape
    assert clips == 1
    rank = lax.axis_index("sp")
    own = width // n_sp
    block = w_q.shape[0]
    hidden = f_up.shape[1]
    unit = f_down.shape[0] // n_sp
    flen, tlen = frame_len, text_len

    def own_cols(weight):
        return lax.dynamic_slice_in_dim(weight, rank * own, own, axis=1)

    def own_rows(rows):
        return lax.dynamic_slice_in_dim(rows, rank * local, local, axis=0)

    def from_dp(part):
        return lax.all_gather(part, "dp", axis=0, tiled=True)

    small = jnp.stack([gain_a, bias_a, gain_c, bias_c, gain_f, bias_f], axis=1)
    small = jnp.pad(small, ((0, 0), (0, 128 - small.shape[1])))
    first = from_dp(jnp.concatenate([own_cols(w) for w in (w_q, w_k, w_v)] + [small], axis=1))
    second = from_dp(jnp.concatenate([own_cols(w) for w in (w_o, c_q, c_o, c_k, c_v)], axis=1))
    down_own = lax.dynamic_slice_in_dim(f_down, rank * unit, unit, axis=0)
    up_own = lax.dynamic_slice_in_dim(
        f_up.reshape(block, n_dp, n_sp, unit), rank, 1, axis=2
    ).reshape(block, n_dp * unit)
    third = from_dp(
        jnp.concatenate([up_own, down_own.reshape(block, unit * width // block)], axis=1)
    )
    up = third[:, : n_dp * unit]
    down = third[:, n_dp * unit :].reshape(n_dp * unit, width)

    qkv_w = first[:, : 3 * own]
    vecs = first[:, 3 * own : 3 * own + 6].astype(F32).T
    ga, ba, gc, bc, gf, bf = (vecs[i : i + 1] for i in range(6))
    o_full, cq_full, co_full = sp_gather(
        n_sp, 2, [second[:, i * own : (i + 1) * own] for i in range(3)], (1, 1, 1)
    )
    cq_own = second[:, own : 2 * own]
    ckv_own = second[:, 3 * own :]

    x, txt, cot = sp_gather(n_sp, 1, [frames[0], text[0], cotangent[0]], (0, 0, 0))
    x = x.astype(F32)

    hat1, _ = norm_parts(x)
    h1 = (hat1 * ga + ba).astype(BF)
    qkv = mm(h1, qkv_w).astype(BF)
    q, k, v = (qkv[:, i * own : (i + 1) * own] for i in range(3))
    ctx_own, lse = attend(q, k, v, flen, True)
    (ctx,) = sp_gather(n_sp, 3, [ctx_own], (1,))
    mid = x + mm(ctx, o_full)
    hat2, inv2 = norm_parts(mid)
    h2 = (hat2 * gc + bc).astype(BF)
    q2 = mm(h2, cq_own).astype(BF)
    kv2 = mm(txt, ckv_own).astype(BF)
    k2, v2 = kv2[:, :own], kv2[:, own:]
    ctx2_own, lse2 = attend(q2, k2, v2, tlen, False)
    (ctx2,) = sp_gather(n_sp, 4, [ctx2_own], (1,))
    after = mid + mm(ctx2, co_full)
    hat3, _ = norm_parts(after)
    h3 = (hat3 * gf + bf).astype(BF)
    u = mm(h3, up)
    act, slope = gelu_parts(u)
    act = act.astype(BF)
    after_own = own_rows(after)
    output = (after_own + sp_scatter(n_sp, 5, mm(act, down))).astype(BF).reshape(frames.shape)

    du = (mm_t(cot, down) * slope).astype(BF)
    part_down = t_mm(act, cot).astype(BF).reshape(n_dp * block, unit * width // block)
    part_ffn = jnp.concatenate([part_down, t_mm(h3, du).astype(BF)], axis=1)
    sum_ffn = lax.psum_scatter(part_ffn, "dp", scatter_dimension=0, tiled=True)
    e3 = sp_scatter(n_sp, 6, mm_t(du, up))
    hat, inv = norm_parts(after_own)
    d_after_own = cotangent[0].astype(F32) + norm_back(e3, hat, inv, gf)
    sums = [jnp.sum(e3 * hat, axis=0), jnp.sum(e3, axis=0)]
    (da2,) = sp_gather(n_sp, 7, [d_after_own.astype(BF)], (0,))
    dctx2 = mm_t(da2, lax.dynamic_slice_in_dim(co_full, rank * own, own, axis=0)).astype(BF)
    dq2, dk2, dv2 = attend_back(q2, k2, v2, dctx2, lse2, tlen, False)
    (dq2_full,) = sp_gather(n_sp, 8, [dq2], (1,))
    part_cross = jnp.concatenate(
        [t_mm(ctx2, own_cols(da2)), t_mm(h2, dq2), t_mm(txt, jnp.concatenate([dk2, dv2], axis=1))],
        axis=1,
    ).astype(BF)
    sum_cross = lax.psum_scatter(part_cross, "dp", scatter_dimension=0, tiled=True)
    grad_text = sp_scatter(n_sp, 9, mm_t(jnp.concatenate([dk2, dv2], axis=1), ckv_own))
    e2 = mm_t(dq2_full, cq_full)
    back2 = norm_back(e2, hat2, inv2, gc)
    da = (da2.astype(F32) + back2).astype(BF)
    e2_own = own_rows(e2)
    hat2_own = own_rows(hat2)
    d_mid_own = d_after_own + own_rows(back2)
    sums = [jnp.sum(e2_own * hat2_own, axis=0), jnp.sum(e2_own, axis=0)] + sums
    dctx = mm_t(da, lax.dynamic_slice_in_dim(o_full, rank * own, own, axis=0)).astype(BF)
    dq, dk, dv = attend_back(q, k, v, dctx, lse, flen, True)
    dqkv = jnp.concatenate([dq, dk, dv], axis=1)
    e1 = sp_scatter(n_sp, 10, mm_t(dqkv, qkv_w))
    hat, inv = norm_parts(frames[0].astype(F32))
    grad_frames = (d_mid_own + norm_back(e1, hat, inv, ga)).reshape(frames.shape)
    sums = [jnp.sum(e1 * hat, axis=0), jnp.sum(e1, axis=0)] + sums
    sums = jnp.pad(jnp.stack(sums, axis=1), ((0, 0), (0, 122)))
    part_self = jnp.concatenate(
        [t_mm(ctx, own_cols(da)), t_mm(h1, dqkv), sums], axis=1
    ).astype(BF)
    sum_self = lax.psum_scatter(part_self, "dp", scatter_dimension=0, tiled=True)

    (done,) = sp_gather(
        n_sp, 11, [jnp.concatenate([sum_ffn, sum_cross, sum_self], axis=1)], (0,)
    )
    done = done.reshape(n_sp, block, done.shape[1]).astype(F32)
    at = unit * width // block
    grad_down = done[:, :, :at].reshape(n_sp * unit, width)
    grad_up = done[:, :, at : at + n_dp * unit].reshape(n_sp, block, n_dp, unit)
    grad_up = jnp.transpose(grad_up, (1, 2, 0, 3)).reshape(block, hidden)
    at += n_dp * unit
    squares = []
    for _ in range(8):
        squares.append(jnp.transpose(done[:, :, at : at + own], (1, 0, 2)).reshape(block, width))
        at += own
    g_co, g_cq, g_ck, g_cv, g_o, g_q, g_k, g_v = squares
    vec = jnp.sum(done[:, :, at : at + 6], axis=0)
    return (
        output, grad_frames, grad_text.reshape(text.shape),
        g_q, g_k, g_v, g_o, g_cq, g_ck, g_cv, g_co, grad_up, grad_down,
    ) + tuple(vec[:, i] for i in range(6))


def solution(mesh):
    rows, flat, vec = P("dp", "sp", None), P("dp", None), P("dp")
    return jax.shard_map(
        partial(on_device, mesh.shape["dp"], mesh.shape["sp"]),
        mesh=mesh,
        in_specs=(rows, rows, vec, vec, rows) + (flat,) * 10 + (vec,) * 6,
        out_specs=(rows, rows, rows) + (flat,) * 10 + (vec,) * 6,
        check_vma=False,
    )
```

time: 1030 us -> 655 us (0.64)
  waiting for transfers between devices: 643 us -> 135 us
  Pallas kernels: 0 us -> 328 us
  matrix products: 181 us -> 84.5 us
  local copies, waits for them, and re-layouts: 94.4 us -> 46.3 us
  other arithmetic: 72.2 us -> 36.1 us
  blocking collectives: 10.5 us -> 0 us
    pallas_call x0 -> x15, Pallas kernels: none -> 328 us  [the longest x7 201 us: sp_gather(): pl.pallas_call(partial(gather_kernel, n_sp, axes), out_shape=tuple(shapes...]
    unnamed x22 -> x6, waiting for transfers between devices: 212 us -> 0.1 us
    all_gather x4 -> x3, waiting for transfers between devices: 183 us -> 4.42 us  [from_dp(): return lax.all_gather(part, 'dp', axis=0, tiled=True)]
    all_gather x8 -> x0, waiting for transfers between devices: 169 us -> none  [the longest x3 74.5 us: gather_rows(): return lax.all_gather(block, 'sp', axis=0, tiled=True)]
    reduce_scatter x4 -> x3, waiting for transfers between devices: 79 us -> 130 us  [the longest x1 91 us: on_device(): sum_ffn = lax.psum_scatter(part_ffn, 'dp', scatter_dimension=0, tiled=True)]
    dot_general x23 -> x7, matrix products: 76.4 us -> 28.4 us  [mm_t(): lax.dot_general(a, b, (((1,), (1,)), ((), ())), preferred_element_type=F32)]
    dot_general x23 -> x7, matrix products: 49.5 us -> 24.1 us  [t_mm(): lax.dot_general(a, b, (((0,), (0,)), ((), ())), preferred_element_type=F32)]
    transpose x13 -> x0, local copies, waits for them, and re-layouts: 23.9 us -> none  [the longest x4 15.9 us: on_device(): jnp.transpose(full3[:, :, i * own:(i + 1) * own], (1, 0, 2))]
  transfers between devices with their start and end apart: 19 -> 6, of which waited for: 18 -> 3; matrix products, arithmetic and copies ran while one was open for 15% -> 14% of each run, Pallas kernels for 0% -> 31%
where the time goes in v2:
time: 655 us; the launch traced here: 647 us
  Pallas kernels  328 us (50%)
  waiting for transfers between devices  135 us (21%)
  matrix products  84.5 us (13%)
  local copies, waits for them, and re-layouts  46.3 us (7%)
  other arithmetic  36.1 us (6%)
  between operations  16.7 us (3%)
    pallas_call x7, Pallas kernels, sp_gather(): pl.pallas_call(partial(gather_kernel, n_sp, axes), out_shape=tuple(shapes...  201 us
    reduce_scatter x1, waiting for transfers between devices, on_device(): sum_ffn = lax.psum_scatter(part_ffn, 'dp', scatter_dimension=0, tiled=True)  91 us
    pallas_call x4, Pallas kernels, sp_scatter(): pl.pallas_call(partial(scatter_kernel, n_sp), out_shape=jax.ShapeDtypeStr...  74.8 us
    reduce_scatter x1, waiting for transfers between devices, on_device(): lax.psum_scatter(part_self, 'dp', scatter_dimension=0, tiled=True)  39.1 us
    dot_general x7, matrix products, mm(): return jnp.dot(a, b, preferred_element_type=F32)  31.9 us
    pallas_call x2, Pallas kernels, attend_back(): pl.pallas_call(partial(attend_back_kernel, causal, STEP), out_shape=(jax....  30.5 us
    dot_general x7, matrix products, mm_t(): lax.dot_general(a, b, (((1,), (1,)), ((), ())), preferred_element_type=F32)  28.4 us
    dot_general x7, matrix products, t_mm(): lax.dot_general(a, b, (((0,), (0,)), ((), ())), preferred_element_type=F32)  24.1 us
  transfers between devices with their start and end apart: 6, of which 3 were waited for; matrix products, arithmetic and copies ran while one was open for 14% of the time, Pallas kernels for 31%

profile of v2, /device:TPU:0, one launch (start us, length us, event | category | flops | bytes accessed | tf_op | source)
XLA Modules:
  0.0 647.0 jit_solution(478373467239215677)
XLA Ops:
  22.0 41.1 %sp_gather.7 = (bf16[1280,1024]{1,0:T(8,128)(2,1)}, bf16[256,1024]{1,0:T(8,128)(2,1)}, bf16[1280,1024]{1,0:T(8,128)(2,1)}) custom-call(bf16[320,1024]{1,0:T(8,128)(2,1)} %bitcast.95, bf16[64,1024]{1,0:T(8,128)(2,1)} %bitcast.112, bf16[320,1024]{1,0:T(8,128)(2,1)} %bitcast.99), custom_call_target="tpu_custom_call" | custom-call | bytes 115343360 | tf_op jit(solution)/shard_map/sp_gather/pallas_call | solution.py:264
  69.3 4.5 convolution_convert_fusion.3
  75.1 14.9 %attend.2 = (bf16[1280,256]{1,0:T(8,128)(2,1)}, f32[8,1280]{1,0:T(8,128)}) custom-call(s32[1]{0:T(128)S(6)} %copy.151.length_ref, bf16[1280,256]{1,0:T(8,128)(2,1)} %get-tuple-element.95.q_ref, bf16[1280,256]{1,0:T(8,128)(2,1)} %get-tuple-element.94.k_ref, bf16[1280,256]{1,0:T(8,128)(2,1)} %get-tuple-element.93.v_ref), custom_call_target="tpu_custom_call" | custom-call | flops 3355443200 | bytes 2621440 | tf_op jit(solution)/shard_map/attend/pallas_call | solution.py:148
  89.9 21.5 %sp_gather.8 = bf16[1280,1024]{1,0:T(8,128)(2,1)} custom-call(bf16[1280,256]{1,0:T(8,128)(2,1)} %get-tuple-element.36.refs_0_), custom_call_target="tpu_custom_call" | custom-call | bytes 52428800 | tf_op jit(solution)/shard_map/sp_gather/pallas_call | solution.py:264
  111.4 4.4 all-gather.6.cloned.1.call-done
  118.5 42.3 %sp_gather.9 = (bf16[1024,1024]{1,0:T(8,128)(2,1)}, bf16[1024,1024]{1,0:T(8,128)(2,1)}, bf16[1024,1024]{1,0:T(8,128)(2,1)}) custom-call(bf16[1024,256]{1,0:T(8,128)(2,1)} %get-tuple-element.92.refs_0_, bf16[1024,256]{1,0:T(8,128)(2,1)} %get-tuple-element.91.refs_1_, bf16[1024,256]{1,0:T(8,128)(2,1)} %get-tuple-element.90.refs_2_), custom_call_target="tpu_custom_call" | custom-call | bytes 125829120 | tf_op jit(solution)/shard_map/sp_gather/pallas_call | solution.py:264
  160.9 5.5 fusion.54
  174.4 7.3 %attend.3 = (bf16[1280,256]{1,0:T(8,128)(2,1)}, f32[8,1280]{1,0:T(8,128)}) custom-call(s32[1]{0:T(128)S(6)} %copy.152.length_ref, bf16[1280,256]{1,0:T(8,128)(2,1)} %convolution_convert_fusion.6.q_ref, bf16[256,256]{1,0:T(8,128)(2,1)} %get-tuple-element.97.k_ref, bf16[256,256]{1,0:T(8,128)(2,1)} %get-tuple-element.96.v_ref), custom_call_target="tpu_custom_call" | custom-call | flops 671088640 | bytes 2621440 | tf_op jit(solution)/shard_map/attend/pallas_call | solution.py:148
  181.6 21.4 %sp_gather.10 = bf16[1280,1024]{1,0:T(8,128)(2,1)} custom-call(bf16[1280,256]{1,0:T(8,128)(2,1)} %get-tuple-element.39.refs_0_), custom_call_target="tpu_custom_call" | custom-call | bytes 52428800 | tf_op jit(solution)/shard_map/sp_gather/pallas_call | solution.py:264
  203.1 6.8 %fusion.55 = (f32[1280]{0:T(1024)S(1)}, f32[1280,1024]{1,0:T(8,128)S(1)}) fusion(f32[1280,1024]{1,0:T(8,128)} %copy-done.2, bf16[1280,1024]{1,0:T(8,128)(2,1)} %sp_gather.10, bf16[1024,1024]{1,0:T(8,128)(2,1)S(1)} %copy-done.38), kind=kOutput, calls=%fused_computation.160 | convolution fusion | flops 2686974720 | bytes 15209472 | tf_op jit(solution)/shard_map/dot_general | solution.py:18
  212.3 6.8 %multiply_convert_fusion = (bf16[1280,1024]{1,0:T(8,128)(2,1)S(1)}, f32[1280,1024]{1,0:T(8,128)S(1)}) fusion(bf16[1024,2048]{1,0:T(8,128)(2,1)} %all-gather.8.cloned.1.call-done, f32[1280,1024]{1,0:T(8,128)} %copy-done.3, f32[1024]{0:T(1024)S(1)} %get-tuple-element.64, f32[1024]{0:T(1024)S(1)} %get-tuple-element.63, f32[1280]{0:T(1024)S(1)} %add_rsqrt_fusion, ...), kind=kOutput, calls=%fused_computation.19 | convolution fusion | flops 2697461760 | bytes 15222784 | tf_op jit(solution)/shard_map/dot_general | solution.py:18
  219.1 4.7 fusion.11
  225.2 4.3 convolution_convert_fusion.1.part_ref
  229.6 22.2 %sp_scatter.5 = f32[320,1024]{1,0:T(8,128)} custom-call(bf16[1280,1024]{1,0:T(8,128)(2,1)} %convolution_convert_fusion.1.part_ref), custom_call_target="tpu_custom_call" | custom-call | bytes 52428800 | tf_op jit(solution)/shard_map/sp_scatter/pallas_call | solution.py:317
  251.7 5.7 convolution_convert_fusion.2.part_ref
  257.5 21.8 %sp_scatter.4 = f32[320,1024]{1,0:T(8,128)} custom-call(bf16[1280,1024]{1,0:T(8,128)(2,1)} %convolution_convert_fusion.2.part_ref), custom_call_target="tpu_custom_call" | custom-call | bytes 52428800 | tf_op jit(solution)/shard_map/sp_scatter/pallas_call | solution.py:317
  281.3 3.4 fusion.49
  284.8 21.3 %sp_gather.11 = bf16[1280,1024]{1,0:T(8,128)(2,1)} custom-call(bf16[320,1024]{1,0:T(8,128)(2,1)} %get-tuple-element.77.refs_0_), custom_call_target="tpu_custom_call" | custom-call | bytes 52428800 | tf_op jit(solution)/shard_map/sp_gather/pallas_call | solution.py:264
  311.8 10.9 %attend_back.2 = (bf16[1280,256]{1,0:T(8,128)(2,1)}, bf16[256,256]{1,0:T(8,128)(2,1)}, bf16[256,256]{1,0:T(8,128)(2,1)}) custom-call(s32[1]{0:T(128)S(6)} %copy.152.length_ref, bf16[1280,256]{1,0:T(8,128)(2,1)} %convolution_convert_fusion.6.q_ref, bf16[256,256]{1,0:T(8,128)(2,1)} %get-tuple-element.97.k_ref, bf16[256,256]{1,0:T(8,128)(2,1)} %get-tuple-element.96.v_ref, ...), custom_call_target="tpu_custom_call" | custom-call | flops 1677721600 | bytes 4587520 | tf_op jit(solution)/shard_map/attend_back/pallas_call | solution.py:169
  322.7 3.6 convolution_convert_fusion.12
  326.3 21.6 %sp_gather.12 = bf16[1280,1024]{1,0:T(8,128)(2,1)} custom-call(bf16[1280,256]{1,0:T(8,128)(2,1)} %get-tuple-element.43.refs_0_), custom_call_target="tpu_custom_call" | custom-call | bytes 52428800 | tf_op jit(solution)/shard_map/sp_gather/pallas_call | solution.py:264
  350.1 7.5 %multiply_reduce_fusion.3 = (f32[1280]{0:T(1024)S(1)}, f32[1280]{0:T(1024)S(1)}, f32[1280,1024]{1,0:T(8,128)S(1)}) fusion(f32[1024]{0:T(1024)S(1)} %get-tuple-element.66, f32[1280,1024]{1,0:T(8,128)} %copy-done.13, bf16[1280,1024]{1,0:T(8,128)(2,1)} %sp_gather.12, bf16[1024,1024]{1,0:T(8,128)(2,1)} %get-tuple-element.44), kind=kOutput, calls=%fused_computation.28 | convolution fusion | flops 2689594880 | bytes 15218688 | tf_op jit(solution)/shard_map/dot_general | solution.py:22
  357.7 3.5 add_convert_fusion
  366.6 19.7 %attend_back.3 = (bf16[1280,256]{1,0:T(8,128)(2,1)}, bf16[1280,256]{1,0:T(8,128)(2,1)}, bf16[1280,256]{1,0:T(8,128)(2,1)}) custom-call(s32[1]{0:T(128)S(6)} %copy.151.length_ref, bf16[1280,256]{1,0:T(8,128)(2,1)} %get-tuple-element.95.q_ref, bf16[1280,256]{1,0:T(8,128)(2,1)} %get-tuple-element.94.k_ref, bf16[1280,256]{1,0:T(8,128)(2,1)} %get-tuple-element.93.v_ref, ...), custom_call_target="tpu_custom_call" | custom-call | flops 8388608000 | bytes 4587520 | tf_op jit(solution)/shard_map/attend_back/pallas_call | solution.py:169
  390.0 3.7 convolution_convert_fusion.part_ref
  393.8 22.2 %sp_scatter.6 = f32[320,1024]{1,0:T(8,128)} custom-call(bf16[1280,1024]{1,0:T(8,128)(2,1)} %convolution_convert_fusion.part_ref), custom_call_target="tpu_custom_call" | custom-call | bytes 52428800 | tf_op jit(solution)/shard_map/sp_scatter/pallas_call | solution.py:317
  426.4 5.6 convolution_convert_fusion.8
  432.0 5.8 convolution_convert_fusion.7
  442.8 8.6 %sp_scatter.7 = f32[64,1024]{1,0:T(8,128)} custom-call(bf16[256,1024]{1,0:T(8,128)(2,1)} %convolution_convert_fusion.14.part_ref), custom_call_target="tpu_custom_call" | custom-call | bytes 10485760 | tf_op jit(solution)/shard_map/sp_scatter/pallas_call | solution.py:317
  454.7 39.1 %reduce-scatter.8.cloned.1.call-done = bf16[128,1152]{1,0:T(8,128)(2,1)} async-done(((bf16[1024,1152]{1,0:T(8,128)(2,1)}), bf16[128,1152]{1,0:T(8,128)(2,1)}) %reduce-scatter.8.cloned.1.call-update) | async-done | bytes 294928 | tf_op jit(solution)/shard_map/reduce_scatter | solution.py:447
  493.9 91.0 %reduce-scatter.4.cloned.1.call-done = bf16[128,2048]{1,0:T(8,128)(2,1)} async-done(((bf16[1024,2048]{1,0:T(8,128)(2,1)}), bf16[128,2048]{1,0:T(8,128)(2,1)}) %reduce-scatter.4.cloned.1.call-update) | async-done | bytes 524304 | tf_op jit(solution)/shard_map/reduce_scatter | solution.py:414
  587.2 31.6 %sp_gather.13 = bf16[512,4224]{1,0:T(8,128)(2,1)} custom-call(bf16[128,4224]{1,0:T(8,128)(2,1)} %pad_maximum_fusion.2.refs_0_), custom_call_target="tpu_custom_call" | custom-call | bytes 86507520 | tf_op jit(solution)/shard_map/sp_gather/pallas_call | solution.py:264
  (196 shorter events, 96.1 us)
Async XLA Ops:
  7.2 12.1 %copy-start = (bf16[512,1024]{1,0:T(8,128)(2,1)S(1)}, bf16[512,1024]{1,0:T(8,128)(2,1)}, u32[]{:S(2)}) copy-start(bf16[512,1024]{1,0:T(8,128)(2,1)} %param.35) | copy-start | bytes 3145732
  7.2 59.3 %all-gather.4.cloned.1.call-start = ((), (), s32[]{:S(2)}) async-start(), calls=%async_computation.3 | async-start | bytes 2064384 | tf_op jit(solution)/shard_map/all_gather | solution.py:360
  10.7 105.1 %all-gather.6.cloned.1.call-start = ((), (), s32[]{:S(2)}) async-start(), calls=%async_computation.4 | async-start | bytes 2949120 | tf_op jit(solution)/shard_map/all_gather | solution.py:360
  15.7 196.5 %all-gather.8.cloned.1.call-start = ((), (), s32[]{:S(2)}) async-start(), calls=%async_computation.5 | async-start | bytes 4718592 | tf_op jit(solution)/shard_map/all_gather | solution.py:360
  15.8 5.7 copy-start.4
  20.1 434.6 %reduce-scatter.6.cloned.1.call-start = ((), (), s32[]{:S(2)}) async-start(), calls=%async_computation.7 | async-start | bytes 2359296 | tf_op jit(solution)/shard_map/reduce_scatter | solution.py:427
  115.8 45.0 %copy-start.9 = (bf16[1280,1024]{1,0:T(8,128)(2,1)S(1)}, bf16[1280,1024]{1,0:T(8,128)(2,1)}, u32[]{:S(2)}) copy-start(bf16[1280,1024]{1,0:T(8,128)(2,1)} %get-tuple-element.35) | copy-start | bytes 7864324
  166.3 4.9 copy-start.2
  174.4 28.7 %copy-start.38 = (bf16[1024,1024]{1,0:T(8,128)(2,1)S(1)}, bf16[1024,1024]{1,0:T(8,128)(2,1)}, u32[]{:S(2)}) copy-start(bf16[1024,1024]{1,0:T(8,128)(2,1)} %get-tuple-element.40) | copy-start | bytes 6291460
  212.2 6.8 %copy-start.36 = (bf16[1024,2048]{1,0:T(8,128)(2,1)S(1)}, bf16[1024,2048]{1,0:T(8,128)(2,1)}, u32[]{:S(2)}) copy-start(bf16[1024,2048]{1,0:T(8,128)(2,1)} %all-gather.8.cloned.1.call-done) | copy-start | bytes 12582916
  212.2 6.8 %copy-start.37 = (bf16[1280,1024]{1,0:T(8,128)(2,1)S(1)}, bf16[1280,1024]{1,0:T(8,128)(2,1)}, u32[]{:S(2)}) copy-start(bf16[1280,1024]{1,0:T(8,128)(2,1)} %get-tuple-element.41) | copy-start | bytes 7864324
  219.0 32.7 %copy-start.39 = (bf16[1280,1024]{1,0:T(8,128)(2,1)}, bf16[1280,1024]{1,0:T(8,128)(2,1)S(1)}, u32[]{:S(2)}) copy-start(bf16[1280,1024]{1,0:T(8,128)(2,1)S(1)} %get-tuple-element.102) | copy-start | bytes 7864324
  257.5 21.8 %copy-start.7 = (f32[320,1024]{1,0:T(8,128)S(1)}, f32[320,1024]{1,0:T(8,128)}, u32[]{:S(2)}) copy-start(f32[320,1024]{1,0:T(8,128)} %sp_scatter.5) | copy-start | bytes 3932164
  257.5 23.8 %copy-start.16 = (bf16[1,320,1024]{2,1,0:T(8,128)(2,1)S(1)}, bf16[1,320,1024]{2,1,0:T(8,128)(2,1)}, u32[]{:S(2)}) copy-start(bf16[1,320,1024]{2,1,0:T(8,128)(2,1)} %param.25) | copy-start | bytes 1966084
  284.8 21.3 %copy-start.15 = (bf16[1280,1024]{1,0:T(8,128)(2,1)S(1)}, bf16[1280,1024]{1,0:T(8,128)(2,1)}, u32[]{:S(2)}) copy-start(bf16[1280,1024]{1,0:T(8,128)(2,1)} %sp_gather.10) | copy-start | bytes 7864324
  326.2 21.6 %copy-start.33 = (bf16[256,256]{1,0:T(8,128)(2,1)S(1)}, bf16[256,256]{1,0:T(8,128)(2,1)}, u32[]{:S(2)}) copy-start(bf16[256,256]{1,0:T(8,128)(2,1)} %get-tuple-element.49) | copy-start | bytes 393220
  326.2 21.6 %copy-start.32 = (bf16[256,256]{1,0:T(8,128)(2,1)S(1)}, bf16[256,256]{1,0:T(8,128)(2,1)}, u32[]{:S(2)}) copy-start(bf16[256,256]{1,0:T(8,128)(2,1)} %get-tuple-element.50) | copy-start | bytes 393220
  326.2 21.6 %copy-start.27 = (bf16[256,1024]{1,0:T(8,128)(2,1)S(1)}, bf16[256,1024]{1,0:T(8,128)(2,1)}, u32[]{:S(2)}) copy-start(bf16[256,1024]{1,0:T(8,128)(2,1)} %get-tuple-element.38) | copy-start | bytes 1572868
  326.3 22.1 %copy-start.28 = (bf16[1024,256]{1,0:T(8,128)(2,1)S(1)}, bf16[1024,256]{1,0:T(8,128)(2,1)}, u32[]{:S(2)}) copy-start(bf16[1024,256]{1,0:T(8,128)(2,1)} %convolution_convert_fusion.13) | copy-start | bytes 1572868
  350.0 143.8 %reduce-scatter.8.cloned.1.call-start = ((), (), s32[]{:S(2)}) async-start(), calls=%async_computation.8 | async-start | bytes 2654208 | tf_op jit(solution)/shard_map/reduce_scatter | solution.py:447
  350.1 7.6 %slice-start = ((s8[5242880]{0:T(1024)(128)(4,1)}), s8[4194304]{0:T(1024)(128)(4,1)S(1)}, s32[]{:S(2)}) async-start(s8[5242880]{0:T(1024)(128)(4,1)} %bitcast.93), calls=%async_computation.9 | async-start | bytes 8388608
  350.1 7.6 %slice-start.1 = ((s8[5242880]{0:T(1024)(128)(4,1)}), s8[1048576]{0:T(1024)(128)(4,1)S(1)}, s32[]{:S(2)}) async-start(s8[5242880]{0:T(1024)(128)(4,1)} %bitcast.93), calls=%async_computation.10 | async-start | bytes 2097152
  350.1 7.6 %copy-start.12 = (bf16[1280,1024]{1,0:T(8,128)(2,1)S(1)}, bf16[1280,1024]{1,0:T(8,128)(2,1)}, u32[]{:S(2)}) copy-start(bf16[1280,1024]{1,0:T(8,128)(2,1)} %sp_gather.11) | copy-start | bytes 7864324
  361.2 5.4 copy-start.17
  393.8 22.3 %copy-start.5 = (bf16[1,320,1024]{2,1,0:T(8,128)(2,1)S(1)}, bf16[1,320,1024]{2,1,0:T(8,128)(2,1)}, u32[]{:S(2)}) copy-start(bf16[1,320,1024]{2,1,0:T(8,128)(2,1)} %param.21) | copy-start | bytes 1966084
  426.0 158.9 %reduce-scatter.4.cloned.1.call-start = ((), (), s32[]{:S(2)}) async-start(), calls=%async_computation.6 | async-start | bytes 4718592 | tf_op jit(solution)/shard_map/reduce_scatter | solution.py:414
  426.3 5.6 copy-start.41
  440.2 11.3 %copy-start.6 = (f32[320,1024]{1,0:T(8,128)S(1)}, f32[320,1024]{1,0:T(8,128)}, u32[]{:S(2)}) copy-start(f32[320,1024]{1,0:T(8,128)} %sp_scatter.6) | copy-start | bytes 3932164
  630.0 5.7 copy-start.21
  630.0 6.5 %copy-start.20 = (f32[4,16,8,256]{3,2,1,0:T(8,128)S(1)}, f32[4,16,8,256]{3,2,1,0:T(8,128)}, u32[]{:S(2)}) copy-start(f32[4,16,8,256]{3,2,1,0:T(8,128)} %get-tuple-element.86) | copy-start | bytes 1572868
  632.0 5.4 copy-start.19
  634.8 5.0 copy-start.1
  (18 other events, 51.8 us)
Sparse Core Ops, SparseCore 0:
  10.8 49.0 all-gather.3
  62.7 53.0 all-gather.5
  118.5 71.4 all-gather.7
  350.2 66.3 reduce-scatter.5
  426.2 67.6 reduce-scatter.7
  497.4 87.5 reduce-scatter.3

commit v3 on v2

--- a/solution.py
+++ b/solution.py
@@ -278,55 +278,111 @@
     )(*blocks)
 
 
-def scatter_kernel(n_sp, part_ref, out_ref, near, chip, far_in, send, recv):
+def scatter_kernel(n_sp, count, *refs):
+    parts, outs = refs[:count], refs[count : 2 * count]
+    nears, chips, fars = (refs[at * count : (at + 1) * count] for at in (2, 3, 4))
+    send, recv = refs[5 * count :]
     me, y, side, partner, n_y = sp_place(n_sp)
-    size = out_ref.shape[0]
-
-    def mine(owner):
-        return part_ref.at[pl.ds(pl.multiple_of(owner * size, size), size)]
+
+    def mine(which, owner):
+        size = outs[which].shape[0]
+        return parts[which].at[pl.ds(pl.multiple_of(owner * size, size), size)]
 
     sp_barrier(n_sp)
-    firsts, seconds = [], []
-    for far in range(1, n_y + 1):
-        row = lax.rem(y + far, n_y)
-        slot = far % n_y
-        firsts.append(
-            remote(mine(row * 2 + 1 - side), near.at[slot], send.at[slot], recv.at[slot], partner)
+    firsts, seconds = {}, {}
+    for which in range(count):
+        for far in range(1, n_y + 1):
+            row = lax.rem(y + far, n_y)
+            slot = far % n_y
+            firsts[which, slot] = remote(
+                mine(which, row * 2 + 1 - side), nears[which].at[slot],
+                send.at[which, slot], recv.at[which, slot], partner,
+            )
+            firsts[which, slot].start()
+    for which in range(count):
+        for far in range(1, n_y):
+            peer = lax.rem(y + far, n_y) * 2 + side
+            firsts[which, far].wait_recv()
+            chips[which][far] = (
+                mine(which, peer)[...].astype(F32) + nears[which][far].astype(F32)
+            ).astype(BF)
+            slot = n_y - 1 + far
+            seconds[which, far] = remote(
+                chips[which].at[far], fars[which].at[far],
+                send.at[which, slot], recv.at[which, slot], peer,
+            )
+            seconds[which, far].start()
+    for which in range(count):
+        firsts[which, 0].wait_recv()
+        outs[which][...] = mine(which, me)[...].astype(F32) + nears[which][0].astype(F32)
+        for far in range(1, n_y):
+            seconds[which, far].wait_recv()
+            outs[which][...] += fars[which][far].astype(F32)
+    for copy in list(firsts.values()) + list(seconds.values()):
+        copy.wait_send()
+
+
+def sp_scatter(n_sp, ident, parts):
+    n_y = n_sp // 2
+    shapes = [(part.shape[0] // n_sp, part.shape[1]) for part in parts]
+    rooms = [pltpu.VMEM((n_y,) + shape, BF) for shape in shapes]
+    sent = sum(part.size for part in parts)
+    return pl.pallas_call(
+        partial(scatter_kernel, n_sp, len(parts)),
+        out_shape=tuple(jax.ShapeDtypeStruct(shape, F32) for shape in shapes),
+        in_specs=[VMEM] * len(parts),
+        out_specs=(VMEM,) * len(parts),
+        scratch_shapes=rooms * 3 + [pltpu.SemaphoreType.DMA((len(parts), n_sp))] * 2,
+        compiler_params=pltpu.CompilerParams(
+            collective_id=ident, has_side_effects=True, vmem_limit_bytes=LIMIT
+        ),
+        cost_estimate=pl.CostEstimate(flops=0, bytes_accessed=40 * sent, transcendentals=0),
+        name="sp_scatter",
+    )(*(part.astype(BF) for part in parts))
+
+
+def dp_sum_kernel(n_dp, in_ref, out_ref, land, send, recv):
+    me = lax.axis_index("dp")
+    barrier = pltpu.get_barrier_semaphore()
+    peers = [lax.rem(me + far, n_dp) for far in range(n_dp)]
+    for peer in peers[1:]:
+        pl.semaphore_signal(barrier, inc=1, device_id={"dp": peer})
+    pl.semaphore_wait(barrier, n_dp - 1)
+    copies = []
+    for far in range(1, n_dp):
+        copies.append(
+            pltpu.make_async_remote_copy(
+                src_ref=in_ref.at[peers[far]], dst_ref=land.at[far],
+                send_sem=send.at[far], recv_sem=recv.at[far], device_id={"dp": peers[far]},
+            )
         )
-        firsts[-1].start()
-    for far in range(1, n_y):
-        peer = lax.rem(y + far, n_y) * 2 + side
-        firsts[far - 1].wait_recv()
-        chip[far] = (mine(peer)[...].astype(F32) + near[far].astype(F32)).astype(BF)
-        slot = n_y - 1 + far
-        seconds.append(remote(chip.at[far], far_in.at[far], send.at[slot], recv.at[slot], peer))
-        seconds[-1].start()
-    firsts[n_y - 1].wait_recv()
-    out_ref[...] = mine(me)[...].astype(F32) + near[0].astype(F32)
-    for far in range(1, n_y):
-        seconds[far - 1].wait_recv()
-        out_ref[...] += far_in[far].astype(F32)
-    for copy in firsts + seconds:
+        copies[-1].start()
+    out_ref[...] = in_ref[me].astype(F32)
+    for far in range(1, n_dp):
+        copies[far - 1].wait_recv()
+        out_ref[...] += land[far].astype(F32)
+    for copy in copies:
         copy.wait_send()
 
 
-def sp_scatter(n_sp, ident, part):
-    rows, width = part.shape
-    size, n_y = rows // n_sp, n_sp // 2
-    room = pltpu.VMEM((n_y, size, width), BF)
+def dp_sum(ident, blocks):
+    n_dp = blocks.shape[0]
     return pl.pallas_call(
-        partial(scatter_kernel, n_sp),
-        out_shape=jax.ShapeDtypeStruct((size, width), F32),
+        partial(dp_sum_kernel, n_dp),
+        out_shape=jax.ShapeDtypeStruct(blocks.shape[1:], F32),
         in_specs=[VMEM],
         out_specs=VMEM,
-        scratch_shapes=[room, room, room]
-        + [pltpu.SemaphoreType.DMA((n_sp,)), pltpu.SemaphoreType.DMA((n_sp,))],
+        scratch_shapes=[
+            pltpu.VMEM(blocks.shape, blocks.dtype),
+            pltpu.SemaphoreType.DMA((n_dp,)),
+            pltpu.SemaphoreType.DMA((n_dp,)),
+        ],
         compiler_params=pltpu.CompilerParams(
             collective_id=ident, has_side_effects=True, vmem_limit_bytes=LIMIT
         ),
-        cost_estimate=pl.CostEstimate(flops=0, bytes_accessed=40 * part.size, transcendentals=0),
-        name="sp_scatter",
-    )(part.astype(BF))
+        cost_estimate=pl.CostEstimate(flops=0, bytes_accessed=20 * blocks.size, transcendentals=0),
+        name="dp_sum",
+    )(blocks)
 
 
 def gelu_parts(u):
@@ -406,26 +462,30 @@
     act, slope = gelu_parts(u)
     act = act.astype(BF)
     after_own = own_rows(after)
-    output = (after_own + sp_scatter(n_sp, 5, mm(act, down))).astype(BF).reshape(frames.shape)
+    output = lax.psum_scatter(
+        mm(act, down).astype(BF), "sp", scatter_dimension=0, tiled=True
+    ).astype(F32)
+    output = (after_own + output).astype(BF).reshape(frames.shape)
 
     du = (mm_t(cot, down) * slope).astype(BF)
     part_down = t_mm(act, cot).astype(BF).reshape(n_dp * block, unit * width // block)
     part_ffn = jnp.concatenate([part_down, t_mm(h3, du).astype(BF)], axis=1)
+    part_ffn, du = lax.optimization_barrier((part_ffn, du))
     sum_ffn = lax.psum_scatter(part_ffn, "dp", scatter_dimension=0, tiled=True)
-    e3 = sp_scatter(n_sp, 6, mm_t(du, up))
+    (e3,) = sp_scatter(n_sp, 6, [mm_t(du, up)])
     hat, inv = norm_parts(after_own)
     d_after_own = cotangent[0].astype(F32) + norm_back(e3, hat, inv, gf)
     sums = [jnp.sum(e3 * hat, axis=0), jnp.sum(e3, axis=0)]
     (da2,) = sp_gather(n_sp, 7, [d_after_own.astype(BF)], (0,))
     dctx2 = mm_t(da2, lax.dynamic_slice_in_dim(co_full, rank * own, own, axis=0)).astype(BF)
     dq2, dk2, dv2 = attend_back(q2, k2, v2, dctx2, lse2, tlen, False)
+    dkv2 = jnp.concatenate([dk2, dv2], axis=1)
+    part_cross = jnp.concatenate(
+        [t_mm(ctx2, own_cols(da2)), t_mm(h2, dq2), t_mm(txt, dkv2)], axis=1
+    ).astype(BF)
+    part_cross, dq2 = lax.optimization_barrier((part_cross, dq2))
+    sum_cross = lax.psum_scatter(part_cross, "dp", scatter_dimension=0, tiled=True)
     (dq2_full,) = sp_gather(n_sp, 8, [dq2], (1,))
-    part_cross = jnp.concatenate(
-        [t_mm(ctx2, own_cols(da2)), t_mm(h2, dq2), t_mm(txt, jnp.concatenate([dk2, dv2], axis=1))],
-        axis=1,
-    ).astype(BF)
-    sum_cross = lax.psum_scatter(part_cross, "dp", scatter_dimension=0, tiled=True)
-    grad_text = sp_scatter(n_sp, 9, mm_t(jnp.concatenate([dk2, dv2], axis=1), ckv_own))
     e2 = mm_t(dq2_full, cq_full)
     back2 = norm_back(e2, hat2, inv2, gc)
     da = (da2.astype(F32) + back2).astype(BF)
@@ -436,35 +496,37 @@
     dctx = mm_t(da, lax.dynamic_slice_in_dim(o_full, rank * own, own, axis=0)).astype(BF)
     dq, dk, dv = attend_back(q, k, v, dctx, lse, flen, True)
     dqkv = jnp.concatenate([dq, dk, dv], axis=1)
-    e1 = sp_scatter(n_sp, 10, mm_t(dqkv, qkv_w))
+    part_self = jnp.concatenate([t_mm(ctx, own_cols(da)), t_mm(h1, dqkv)], axis=1).astype(BF)
+    part_self, dqkv = lax.optimization_barrier((part_self, dqkv))
+    sum_self = lax.psum_scatter(part_self, "dp", scatter_dimension=0, tiled=True)
+    e1, grad_text = sp_scatter(n_sp, 10, [mm_t(dqkv, qkv_w), mm_t(dkv2, ckv_own)])
     hat, inv = norm_parts(frames[0].astype(F32))
     grad_frames = (d_mid_own + norm_back(e1, hat, inv, ga)).reshape(frames.shape)
     sums = [jnp.sum(e1 * hat, axis=0), jnp.sum(e1, axis=0)] + sums
-    sums = jnp.pad(jnp.stack(sums, axis=1), ((0, 0), (0, 122)))
-    part_self = jnp.concatenate(
-        [t_mm(ctx, own_cols(da)), t_mm(h1, dqkv), sums], axis=1
-    ).astype(BF)
-    sum_self = lax.psum_scatter(part_self, "dp", scatter_dimension=0, tiled=True)
-
-    (done,) = sp_gather(
-        n_sp, 11, [jnp.concatenate([sum_ffn, sum_cross, sum_self], axis=1)], (0,)
-    )
+    sums = jnp.transpose(jnp.stack(sums).reshape(6, n_dp, block), (1, 0, 2))
+    sums = jnp.pad(sums, ((0, 0), (0, 2), (0, 128 - block)))
+    vec = dp_sum(12, sums)
+    sum_ffn, sum_cross, vec = lax.optimization_barrier((sum_ffn, sum_cross, vec))
+    done, = sp_gather(n_sp, 11, [jnp.concatenate([sum_ffn, sum_cross], axis=1)], (0,))
+    last, vec = sp_gather(n_sp, 13, [sum_self, vec], (0, 0))
     done = done.reshape(n_sp, block, done.shape[1]).astype(F32)
+    last = last.reshape(n_sp, block, last.shape[1]).astype(F32)
+    vec = jnp.sum(vec.reshape(n_sp, 8, 128), axis=0)[:6, :block]
     at = unit * width // block
     grad_down = done[:, :, :at].reshape(n_sp * unit, width)
     grad_up = done[:, :, at : at + n_dp * unit].reshape(n_sp, block, n_dp, unit)
     grad_up = jnp.transpose(grad_up, (1, 2, 0, 3)).reshape(block, hidden)
     at += n_dp * unit
-    squares = []
-    for _ in range(8):
-        squares.append(jnp.transpose(done[:, :, at : at + own], (1, 0, 2)).reshape(block, width))
-        at += own
-    g_co, g_cq, g_ck, g_cv, g_o, g_q, g_k, g_v = squares
-    vec = jnp.sum(done[:, :, at : at + 6], axis=0)
+
+    def square(rows, at):
+        return jnp.transpose(rows[:, :, at : at + own], (1, 0, 2)).reshape(block, width)
+
+    g_co, g_cq, g_ck, g_cv = (square(done, at + i * own) for i in range(4))
+    g_o, g_q, g_k, g_v = (square(last, i * own) for i in range(4))
     return (
         output, grad_frames, grad_text.reshape(text.shape),
         g_q, g_k, g_v, g_o, g_cq, g_ck, g_cv, g_co, grad_up, grad_down,
-    ) + tuple(vec[:, i] for i in range(6))
+    ) + tuple(vec[i] for i in range(6))
 
 
 def solution(mesh):

time: 655 us -> 537 us (0.82)
  waiting for transfers between devices: 135 us -> 23.4 us
  Pallas kernels: 328 us -> 312 us
  other arithmetic: 36.1 us -> 46.6 us
    reduce_scatter x1, waiting for transfers between devices: 91 us -> 0.01 us  [on_device(): sum_ffn = lax.psum_scatter(part_ffn, 'dp', scatter_dimension=0, tiled=True)]
    reduce_scatter x1, waiting for transfers between devices: 39.1 us -> 17.1 us  [on_device(): lax.psum_scatter(part_self, 'dp', scatter_dimension=0, tiled=True)]
    pallas_call x4 -> x3, Pallas kernels: 74.8 us -> 55.5 us  [the longest x2 47.4 us: sp_scatter(): pl.pallas_call(partial(scatter_kernel, n_sp, len(parts)), out_shape=tuple...]
    dot_general x7, matrix products: 24.1 us -> 17.2 us  [t_mm(): lax.dot_general(a, b, (((0,), (0,)), ((), ())), preferred_element_type=F32)]
    pallas_call x7 -> x8, Pallas kernels: 201 us -> 204 us  [sp_gather(): pl.pallas_call(partial(gather_kernel, n_sp, axes), out_shape=tuple(shapes...]
    unnamed x100 -> x83, local copies, waits for them, and re-layouts: 17.8 us -> 20.7 us
  transfers between devices with their start and end apart: 6 -> 7, of which waited for: 3 -> 2; matrix products, arithmetic and copies ran while one was open for 14% -> 25% of each run, Pallas kernels for 31% -> 57%
where the time goes in v3:
time: 537 us; the launch traced here: 530 us
  Pallas kernels  312 us (58%)
  matrix products  82.9 us (15%)
  local copies, waits for them, and re-layouts  47.8 us (9%)
  other arithmetic  46.6 us (9%)
  waiting for transfers between devices  23.4 us (4%)
  between operations  16.7 us (3%)
    pallas_call x8, Pallas kernels, sp_gather(): pl.pallas_call(partial(gather_kernel, n_sp, axes), out_shape=tuple(shapes...  204 us
    pallas_call x2, Pallas kernels, sp_scatter(): pl.pallas_call(partial(scatter_kernel, n_sp, len(parts)), out_shape=tuple...  47.4 us
    dot_general x7, matrix products, mm_t(): lax.dot_general(a, b, (((1,), (1,)), ((), ())), preferred_element_type=F32)  33.9 us
    dot_general x7, matrix products, mm(): return jnp.dot(a, b, preferred_element_type=F32)  31.8 us
    pallas_call x2, Pallas kernels, attend_back(): pl.pallas_call(partial(attend_back_kernel, causal, STEP), out_shape=(jax....  30.8 us
    pallas_call x2, Pallas kernels, attend(): pl.pallas_call(partial(attend_kernel, causal, STEP), out_shape=(jax.Shape...  22 us
    unnamed x83, local copies, waits for them, and re-layouts  20.7 us
    dot_general x7, matrix products, t_mm(): lax.dot_general(a, b, (((0,), (0,)), ((), ())), preferred_element_type=F32)  17.2 us
  transfers between devices with their start and end apart: 7, of which 2 were waited for; matrix products, arithmetic and copies ran while one was open for 25% of the time, Pallas kernels for 57%

profile of v3, /device:TPU:0, one launch (start us, length us, event | category | flops | bytes accessed | tf_op | source)
XLA Modules:
  0.0 529.9 jit_solution(18309081549363933423)
XLA Ops:
  20.5 41.1 %sp_gather.8 = (bf16[1280,1024]{1,0:T(8,128)(2,1)}, bf16[256,1024]{1,0:T(8,128)(2,1)}, bf16[1280,1024]{1,0:T(8,128)(2,1)}) custom-call(bf16[320,1024]{1,0:T(8,128)(2,1)} %bitcast.119, bf16[64,1024]{1,0:T(8,128)(2,1)} %bitcast.140, bf16[320,1024]{1,0:T(8,128)(2,1)} %bitcast.125), custom_call_target="tpu_custom_call" | custom-call | bytes 115343360 | tf_op jit(solution)/shard_map/sp_gather/pallas_call | solution.py:264
  67.7 4.5 convolution_convert_fusion.3
  73.5 14.9 %attend.2 = (bf16[1280,256]{1,0:T(8,128)(2,1)}, f32[8,1280]{1,0:T(8,128)}) custom-call(s32[1]{0:T(128)S(6)} %copy.107.length_ref, bf16[1280,256]{1,0:T(8,128)(2,1)} %get-tuple-element.115.q_ref, bf16[1280,256]{1,0:T(8,128)(2,1)} %get-tuple-element.114.k_ref, bf16[1280,256]{1,0:T(8,128)(2,1)} %get-tuple-element.113.v_ref), custom_call_target="tpu_custom_call" | custom-call | flops 3355443200 | bytes 2621440 | tf_op jit(solution)/shard_map/attend/pallas_call | solution.py:148
  88.4 21.4 %sp_gather.9 = bf16[1280,1024]{1,0:T(8,128)(2,1)} custom-call(bf16[1280,256]{1,0:T(8,128)(2,1)} %get-tuple-element.49.refs_0_), custom_call_target="tpu_custom_call" | custom-call | bytes 52428800 | tf_op jit(solution)/shard_map/sp_gather/pallas_call | solution.py:264
  109.8 6.1 %all-gather.6.cloned.1.call-done = bf16[1024,1280]{1,0:T(8,128)(2,1)} async-done(((bf16[128,1280]{1,0:T(8,128)(2,1)}), bf16[1024,1280]{1,0:T(8,128)(2,1)}) %all-gather.6.cloned.1.call-update) | async-done | bytes 2621456 | tf_op jit(solution)/shard_map/all_gather | solution.py:416
  118.6 42.3 %sp_gather.10 = (bf16[1024,1024]{1,0:T(8,128)(2,1)}, bf16[1024,1024]{1,0:T(8,128)(2,1)}, bf16[1024,1024]{1,0:T(8,128)(2,1)}) custom-call(bf16[1024,256]{1,0:T(8,128)(2,1)} %get-tuple-element.108.refs_0_, bf16[1024,256]{1,0:T(8,128)(2,1)} %get-tuple-element.107.refs_1_, bf16[1024,256]{1,0:T(8,128)(2,1)} %get-tuple-element.106.refs_2_), custom_call_target="tpu_custom_call" | custom-call | bytes 125829120 | tf_op jit(solution)/shard_map/sp_gather/pallas_call | solution.py:264
  160.9 5.5 %fusion.52 = (f32[1280]{0:T(1024)S(1)}, f32[1280,1024]{1,0:T(8,128)S(1)}) fusion(bf16[1280,1024]{1,0:T(8,128)(2,1)} %sp_gather.9, bf16[1024,1024]{1,0:T(8,128)(2,1)} %get-tuple-element.50, bf16[1280,1024]{1,0:T(8,128)(2,1)S(1)} %copy-done.8), kind=kOutput, calls=%fused_computation.156 | convolution fusion | flops 2688285440 | bytes 12588032 | tf_op jit(solution)/shard_map/dot_general | solution.py:18
  174.4 7.1 %attend.3 = (bf16[1280,256]{1,0:T(8,128)(2,1)}, f32[8,1280]{1,0:T(8,128)}) custom-call(s32[1]{0:T(128)S(6)} %copy.108.length_ref, bf16[1280,256]{1,0:T(8,128)(2,1)} %convolution_convert_fusion.6.q_ref, bf16[256,256]{1,0:T(8,128)(2,1)} %get-tuple-element.117.k_ref, bf16[256,256]{1,0:T(8,128)(2,1)} %get-tuple-element.116.v_ref), custom_call_target="tpu_custom_call" | custom-call | flops 671088640 | bytes 2621440 | tf_op jit(solution)/shard_map/attend/pallas_call | solution.py:148
  181.5 21.4 %sp_gather.11 = bf16[1280,1024]{1,0:T(8,128)(2,1)} custom-call(bf16[1280,256]{1,0:T(8,128)(2,1)} %get-tuple-element.52.refs_0_), custom_call_target="tpu_custom_call" | custom-call | bytes 52428800 | tf_op jit(solution)/shard_map/sp_gather/pallas_call | solution.py:264
  202.9 6.9 %fusion.53 = (f32[1280]{0:T(1024)S(1)}, f32[1280,1024]{1,0:T(8,128)S(1)}) fusion(f32[1280,1024]{1,0:T(8,128)} %copy-done.2, bf16[1280,1024]{1,0:T(8,128)(2,1)} %sp_gather.11, bf16[1024,1024]{1,0:T(8,128)(2,1)} %get-tuple-element.53), kind=kOutput, calls=%fused_computation.157 | convolution fusion | flops 2686974720 | bytes 15209472 | tf_op jit(solution)/shard_map/dot_general | solution.py:18
  212.2 8.1 %multiply_convert_fusion = (bf16[1280,1024]{1,0:T(8,128)(2,1)S(1)}, f32[1280,1024]{1,0:T(8,128)}) fusion(bf16[1024,2048]{1,0:T(8,128)(2,1)} %all-gather.8.cloned.1.call-done, f32[1280,1024]{1,0:T(8,128)} %copy-done.4, f32[1024]{0:T(1024)S(1)} %get-tuple-element.90, f32[1024]{0:T(1024)S(1)} %get-tuple-element.89, f32[1280]{0:T(1024)S(1)} %add_rsqrt_fusion, ...), kind=kOutput, calls=%fused_computation.19 | convolution fusion | flops 2697461760 | bytes 15222784 | tf_op jit(solution)/shard_map/dot_general | solution.py:18
  221.8 4.2 convolution_convert_fusion.2
  226.2 5.6 %convolution_convert_fusion.8 = bf16[1024,1024]{1,0:T(8,128)(2,1)S(1)} fusion(bf16[1280,1024]{1,0:T(8,128)(2,1)} %copy-done.28, bf16[1280,1024]{1,0:T(8,128)(2,1)} %get-tuple-element.54), kind=kOutput, calls=%fused_computation.40 | convolution fusion | flops 2685403136 | bytes 7340032 | tf_op jit(solution)/shard_map/dot_general | solution.py:26
  233.4 4.5 fusion.11
  237.9 3.4 convolution_convert_fusion.7
  247.1 6.8 %convolution_convert_fusion.1.refs_0_ = bf16[1280,1024]{1,0:T(8,128)(2,1)} fusion(bf16[1280,1024]{1,0:T(8,128)(2,1)} %copy-done.30, bf16[1024,2048]{1,0:T(8,128)(2,1)} %all-gather.8.cloned.1.call-done), kind=kOutput, calls=%fused_computation.30 | convolution fusion | flops 2685665280 | bytes 7340032 | tf_op jit(solution)/shard_map/dot_general | solution.py:22
  253.9 22.2 %sp_scatter.2 = f32[320,1024]{1,0:T(8,128)} custom-call(bf16[1280,1024]{1,0:T(8,128)(2,1)} %convolution_convert_fusion.1.refs_0_), custom_call_target="tpu_custom_call" | custom-call | bytes 52428800 | tf_op jit(solution)/shard_map/sp_scatter/pallas_call | solution.py:330
  278.6 3.6 fusion.47
  282.2 21.1 %sp_gather.12 = bf16[1280,1024]{1,0:T(8,128)(2,1)} custom-call(bf16[320,1024]{1,0:T(8,128)(2,1)} %get-tuple-element.97.refs_0_), custom_call_target="tpu_custom_call" | custom-call | bytes 52428800 | tf_op jit(solution)/shard_map/sp_gather/pallas_call | solution.py:264
  303.4 3.6 convolution_convert_fusion.5.d_ref
  307.0 11.0 %attend_back.2 = (bf16[1280,256]{1,0:T(8,128)(2,1)}, bf16[256,256]{1,0:T(8,128)(2,1)}, bf16[256,256]{1,0:T(8,128)(2,1)}) custom-call(s32[1]{0:T(128)S(6)} %copy.108.length_ref, bf16[1280,256]{1,0:T(8,128)(2,1)} %convolution_convert_fusion.6.q_ref, bf16[256,256]{1,0:T(8,128)(2,1)} %get-tuple-element.117.k_ref, bf16[256,256]{1,0:T(8,128)(2,1)} %get-tuple-element.116.v_ref, ...), custom_call_target="tpu_custom_call" | custom-call | flops 1677721600 | bytes 4587520 | tf_op jit(solution)/shard_map/attend_back/pallas_call | solution.py:169
  326.0 21.3 %sp_gather.13 = bf16[1280,1024]{1,0:T(8,128)(2,1)} custom-call(bf16[1280,256]{1,0:T(8,128)(2,1)} %get-tuple-element.60.refs_0_), custom_call_target="tpu_custom_call" | custom-call | bytes 52428800 | tf_op jit(solution)/shard_map/sp_gather/pallas_call | solution.py:264
  347.3 9.6 %multiply_reduce_fusion.3 = (f32[1280]{0:T(1024)S(1)}, f32[1280]{0:T(1024)S(1)}, f32[1280,1024]{1,0:T(8,128)}) fusion(f32[1024]{0:T(1024)S(1)} %get-tuple-element.92, f32[1280,1024]{1,0:T(8,128)} %copy-done.10, bf16[1280,1024]{1,0:T(8,128)(2,1)} %sp_gather.13, bf16[1024,1024]{1,0:T(8,128)(2,1)} %get-tuple-element.61), kind=kOutput, calls=%fused_computation.26 | convolution fusion | flops 2689594880 | bytes 15218688 | tf_op jit(solution)/shard_map/dot_general | solution.py:22
  357.0 7.7 %add_convert_fusion = (bf16[1280,1024]{1,0:T(8,128)(2,1)S(1)}, f32[1280,1024]{1,0:T(8,128)}) fusion(bf16[1280,1024]{1,0:T(8,128)(2,1)} %sp_gather.12, f32[1280]{0:T(1024)S(1)} %broadcast_multiply_fusion, f32[1280]{0:T(1024)S(1)} %broadcast_multiply_fusion.1, f32[1280,1024]{1,0:T(8,128)} %get-tuple-element.130, f32[1024]{0:T(1024)S(1)} %get-tuple-element.92, ...), kind=kLoop, calls=%fused_computation.16 | loop fusion | flops 13107200 | bytes 20996096 | tf_op jit(solution)/shard_map/convert_element_type | solution.py:491
  367.5 19.8 %attend_back.3 = (bf16[1280,256]{1,0:T(8,128)(2,1)}, bf16[1280,256]{1,0:T(8,128)(2,1)}, bf16[1280,256]{1,0:T(8,128)(2,1)}) custom-call(s32[1]{0:T(128)S(6)} %copy.107.length_ref, bf16[1280,256]{1,0:T(8,128)(2,1)} %get-tuple-element.115.q_ref, bf16[1280,256]{1,0:T(8,128)(2,1)} %get-tuple-element.114.k_ref, bf16[1280,256]{1,0:T(8,128)(2,1)} %get-tuple-element.113.v_ref, ...), custom_call_target="tpu_custom_call" | custom-call | flops 8388608000 | bytes 4587520 | tf_op jit(solution)/shard_map/attend_back/pallas_call | solution.py:169
  401.1 3.8 convolution_convert_fusion.refs_0_
  404.9 25.2 %sp_scatter.3 = (f32[320,1024]{1,0:T(8,128)}, f32[64,1024]{1,0:T(8,128)}) custom-call(bf16[1280,1024]{1,0:T(8,128)(2,1)} %convolution_convert_fusion.refs_0_, bf16[256,1024]{1,0:T(8,128)(2,1)} %convolution_convert_fusion.11.refs_1_), custom_call_target="tpu_custom_call" | custom-call | bytes 62914560 | tf_op jit(solution)/shard_map/sp_scatter/pallas_call | solution.py:330
  433.6 8.1 %dp_sum.1.refs_1_ = f32[8,128]{1,0:T(8,128)} custom-call(f32[8,8,128]{2,1,0:T(8,128)} %pad.9.in_ref), custom_call_target="tpu_custom_call" | custom-call | bytes 163840 | tf_op jit(solution)/shard_map/dp_sum/pallas_call | solution.py:370
  447.1 23.5 %sp_gather.15 = bf16[512,3072]{1,0:T(8,128)(2,1)} custom-call(bf16[128,3072]{1,0:T(8,128)(2,1)} %pad_maximum_fusion.3.refs_0_), custom_call_target="tpu_custom_call" | custom-call | bytes 62914560 | tf_op jit(solution)/shard_map/sp_gather/pallas_call | solution.py:264
  470.7 5.5 %convert.24 = f32[4,128,3072]{2,1,0:T(8,128)} convert(bf16[4,128,3072]{2,1,0:T(8,128)(2,1)} %bitcast.115) | non-fusion elementwise | flops 1572864 | bytes 9437184 | tf_op jit(solution)/shard_map/convert_element_type | solution.py:512
  477.9 17.1 %reduce-scatter.7.cloned.1.call-done.refs_0_ = bf16[128,1024]{1,0:T(8,128)(2,1)} async-done(((bf16[1024,1024]{1,0:T(8,128)(2,1)}), bf16[128,1024]{1,0:T(8,128)(2,1)}) %reduce-scatter.7.cloned.1.call-update) | async-done | bytes 262160 | tf_op jit(solution)/shard_map/reduce_scatter | solution.py:501
  495.0 11.7 %sp_gather.14 = (bf16[512,1024]{1,0:T(8,128)(2,1)}, f32[32,128]{1,0:T(8,128)}) custom-call(bf16[128,1024]{1,0:T(8,128)(2,1)} %reduce-scatter.7.cloned.1.call-done.refs_0_, f32[8,128]{1,0:T(8,128)} %dp_sum.1.refs_1_), custom_call_target="tpu_custom_call" | custom-call | bytes 21299200 | tf_op jit(solution)/shard_map/sp_gather/pallas_call | solution.py:264
  (178 shorter events, 94.6 us)
Async XLA Ops:
  7.2 11.0 %copy-start = (bf16[512,1024]{1,0:T(8,128)(2,1)S(1)}, bf16[512,1024]{1,0:T(8,128)(2,1)}, u32[]{:S(2)}) copy-start(bf16[512,1024]{1,0:T(8,128)(2,1)} %param.35) | copy-start | bytes 3145732
  7.2 8.6 %copy-start.15 = (bf16[128,4096]{1,0:T(8,128)(2,1)S(1)}, bf16[128,4096]{1,0:T(8,128)(2,1)}, u32[]{:S(2)}) copy-start(bf16[128,4096]{1,0:T(8,128)(2,1)} %param.34) | copy-start | bytes 3145732
  7.2 57.8 %all-gather.4.cloned.1.call-start = ((), (), s32[]{:S(2)}) async-start(), calls=%async_computation.4 | async-start | bytes 2064384 | tf_op jit(solution)/shard_map/all_gather | solution.py:416
  10.8 105.1 %all-gather.6.cloned.1.call-start = ((), (), s32[]{:S(2)}) async-start(), calls=%async_computation.5 | async-start | bytes 2949120 | tf_op jit(solution)/shard_map/all_gather | solution.py:416
  15.8 196.4 %all-gather.8.cloned.1.call-start = ((), (), s32[]{:S(2)}) async-start(), calls=%async_computation.6 | async-start | bytes 4718592 | tf_op jit(solution)/shard_map/all_gather | solution.py:416
  19.1 259.5 %reduce-scatter.5.cloned.1.call-start = ((), (), s32[]{:S(2)}) async-start(), calls=%async_computation.7 | async-start | bytes 3276800 | tf_op jit(solution)/shard_map/reduce_scatter | solution.py:465
  65.0 2.7 copy-start.23
  115.9 45.0 %copy-start.8 = (bf16[1280,1024]{1,0:T(8,128)(2,1)S(1)}, bf16[1280,1024]{1,0:T(8,128)(2,1)}, u32[]{:S(2)}) copy-start(bf16[1280,1024]{1,0:T(8,128)(2,1)} %get-tuple-element.48) | copy-start | bytes 7864324
  166.4 4.9 copy-start.2
  166.4 3.6 copy-start.16
  166.4 3.7 copy-start.18
  212.2 9.6 %copy-start.25 = (bf16[1024,2048]{1,0:T(8,128)(2,1)S(1)}, bf16[1024,2048]{1,0:T(8,128)(2,1)}, u32[]{:S(2)}) copy-start(bf16[1024,2048]{1,0:T(8,128)(2,1)} %all-gather.8.cloned.1.call-done) | copy-start | bytes 12582916
  226.1 219.0 %reduce-scatter.9.cloned.1.call-start = ((), (), s32[]{:S(2)}) async-start(), calls=%async_computation.9 | async-start | bytes 4718592 | tf_op jit(solution)/shard_map/reduce_scatter | solution.py:474
  226.1 5.7 %copy-start.26 = (bf16[1024,2048]{1,0:T(8,128)(2,1)S(1)}, bf16[1024,2048]{1,0:T(8,128)(2,1)}, u32[]{:S(2)}) copy-start(bf16[1024,2048]{1,0:T(8,128)(2,1)} %all-gather.8.cloned.1.call-done) | copy-start | bytes 12582916
  226.1 5.7 %copy-start.27 = (bf16[1280,1024]{1,0:T(8,128)(2,1)S(1)}, bf16[1280,1024]{1,0:T(8,128)(2,1)}, u32[]{:S(2)}) copy-start(bf16[1280,1024]{1,0:T(8,128)(2,1)} %get-tuple-element.54) | copy-start | bytes 7864324
  226.1 7.2 %copy-start.29 = (f32[1280,1024]{1,0:T(8,128)S(1)}, f32[1280,1024]{1,0:T(8,128)}, u32[]{:S(2)}) copy-start(f32[1280,1024]{1,0:T(8,128)} %get-tuple-element.129) | copy-start | bytes 15728644
  226.2 11.7 %slice-start = ((s8[5242880]{0:T(1024)(128)(4,1)}), s8[4194304]{0:T(1024)(128)(4,1)S(1)}, s32[]{:S(2)}) async-start(s8[5242880]{0:T(1024)(128)(4,1)} %bitcast.117), calls=%async_computation.11 | async-start | bytes 8388608
  233.3 4.5 slice-start.1
  237.9 3.4 copy-start.30
  243.7 201.3 %reduce-scatter.11.cloned.1.call-start = ((), (), s32[]{:S(2)}) async-start(), calls=%async_computation.10 | async-start | bytes 2359296 | tf_op jit(solution)/shard_map/reduce_scatter | solution.py:487
  253.9 24.7 %copy-start.13 = (bf16[1,320,1024]{2,1,0:T(8,128)(2,1)S(1)}, bf16[1,320,1024]{2,1,0:T(8,128)(2,1)}, u32[]{:S(2)}) copy-start(bf16[1,320,1024]{2,1,0:T(8,128)(2,1)} %param.25) | copy-start | bytes 1966084
  307.0 16.5 %slice-start.2 = ((s8[5242880]{0:T(1024)(128)(4,1)}), s8[1048576]{0:T(1024)(128)(4,1)S(1)}, s32[]{:S(2)}) async-start(s8[5242880]{0:T(1024)(128)(4,1)} %bitcast.123), calls=%async_computation.13 | async-start | bytes 2097152
  319.8 3.6 slice-start.3
  320.3 3.2 copy-start.17
  356.9 138.1 %reduce-scatter.7.cloned.1.call-start = ((), (), s32[]{:S(2)}) async-start(), calls=%async_computation.8 | async-start | bytes 2359296 | tf_op jit(solution)/shard_map/reduce_scatter | solution.py:501
  387.3 3.6 copy-start.14
  397.8 3.4 copy-start.22
  397.8 3.3 copy-start.24
  430.1 11.6 %copy-start.11 = (f32[320,1024]{1,0:T(8,128)S(1)}, f32[320,1024]{1,0:T(8,128)}, u32[]{:S(2)}) copy-start(f32[320,1024]{1,0:T(8,128)} %get-tuple-element.98) | copy-start | bytes 3932164
  470.6 5.5 %copy-start.3 = (bf16[512,3072]{1,0:T(8,128)(2,1)S(1)}, bf16[512,3072]{1,0:T(8,128)(2,1)}, u32[]{:S(2)}) copy-start(bf16[512,3072]{1,0:T(8,128)(2,1)} %sp_gather.15) | copy-start | bytes 9437188
  516.7 5.9 %copy-start.1 = (bf16[512,1024]{1,0:T(8,128)(2,1)S(1)}, bf16[512,1024]{1,0:T(8,128)(2,1)}, u32[]{:S(2)}) copy-start(bf16[512,1024]{1,0:T(8,128)(2,1)} %param.35) | copy-start | bytes 3145732
  518.5 3.4 copy-start.20
  (10 other events, 19.8 us)
Sparse Core Ops, SparseCore 0:
  10.9 49.0 all-gather.3
  62.8 53.0 all-gather.5
  118.6 71.3 all-gather.7
  226.2 32.1 reduce-scatter.4
  261.9 88.2 reduce-scatter.8
  357.0 66.0 reduce-scatter.10
  427.2 67.7 reduce-scatter.6
